TPU v7x, 32 devices: a whole 2x2x4 slice. The times are simulated.
32 devices in a mesh: ctx: 4 (over z), exp: 8 (over y, x, core).
Axes of the slice: x: 2, y: 2, z: 4, core: 2. Of those that a mesh axis runs over, the one named last changes fastest.
Arguments:
- seq_inputs: bfloat16 [2048, 2048], P('ctx', 'exp'), may hold values from -6 to 6
- step_size: float32 [32, 2048], P('exp', 'ctx'), may hold values from 0.0007 to 0.14
- write_map: bfloat16 [16, 2048], P(None, 'ctx'), may hold values from -2 to 2
- read_map: bfloat16 [16, 2048], P(None, 'ctx'), may hold values from -2 to 2
- decay_log: float32 [32], P('exp'), may hold values from -9.3 to 1.4
- skip_gain: float32 [32], P('exp'), may hold values from 0.5 to 1.5
- moe_tokens: bfloat16 [1024, 4096], P('exp'), may hold values from -6 to 6
- expert_ids: int32 [1024, 2], P('exp'), may hold values from 0 to 3, all different within a row; in each aligned block of 128 rows (0 to 127, 128 to 255, ...) at most 128 rows name the same one
- route_weights: float32 [1024, 2], P('exp'), may hold values from 0.1 to 1
- gate_proj: bfloat16 [8, 4096, 3584], P('exp', None, 'ctx'), may hold values from -0.09375 to 0.09375
- up_proj: bfloat16 [8, 4096, 3584], P('exp', None, 'ctx'), may hold values from -0.09375 to 0.09375
- down_proj: bfloat16 [8, 3584, 4096], P('exp', None, 'ctx'), may hold values from -0.0625 to 0.0625
Outputs:
- mixer_output: bfloat16 [2048, 2048], P('ctx', 'exp')
- expert_output: bfloat16 [1024, 4096], P('exp', 'ctx')
Inputs may be any that keep to these rules, and one draw needn't show every extreme that they name: `expert_ids`: each row names two different experts. In the 128 rows of one index of exp (aligned blocks), no expert is named more than 128 times, and in some blocks an expert is named exactly 128 times.
All inputs are finite; a program needn't handle non-finite values.
Results may differ from a plain program's by a relative error of at most 0.002.
The roundings to bfloat16 on the way count: a program that leaves them out, or rounds other values in their place, can miss the bound.
Values may be sent and summed in bfloat16 or wider, within the bound.
A program may use at most 64 MiB of HBM per device.

v0:
```python
import functools

import jax
import jax.numpy as jnp
from jax import lax
from jax.experimental import pallas as pl
from jax.experimental.pallas import tpu as pltpu
from jax.sharding import PartitionSpec as P

BLOCK = 256


HIGHEST = lax.Precision.HIGHEST


def block_chain(running, pieces):
    decay, increment = pieces
    return (decay[:, None, None] * running + increment, running)


def mixer_prepare(seq_inputs, step_size, write_map, read_map, decay_log):
    length = seq_inputs.shape[0]
    head_count = step_size.shape[0]
    state_count = write_map.shape[0]
    head_width = seq_inputs.shape[1] // head_count
    block_count = length // BLOCK
    decay_rate = -jnp.exp(decay_log)
    log_decay = (step_size * decay_rate[:, None]).reshape(head_count, block_count, BLOCK)
    order = lax.broadcasted_iota(jnp.int32, (BLOCK, BLOCK), 0)
    until = (order <= lax.broadcasted_iota(jnp.int32, (BLOCK, BLOCK), 1)).astype(jnp.float32)
    cumulative = jnp.einsum("hks,st->hkt", log_decay, until, precision=HIGHEST)
    block_ends = cumulative[:, :, BLOCK - 1]
    step_blocks = step_size.reshape(head_count, block_count, BLOCK)
    write_blocks = write_map.reshape(state_count, block_count, BLOCK)
    read_blocks = read_map.reshape(state_count, block_count, BLOCK)
    value_blocks = seq_inputs.reshape(block_count, BLOCK, head_count, head_width)
    scores = jnp.einsum(
        "nkt,nks->kts", read_blocks, write_blocks, preferred_element_type=jnp.float32
    )
    row_index = lax.broadcasted_iota(jnp.int32, (BLOCK, BLOCK), 0)
    column_index = lax.broadcasted_iota(jnp.int32, (BLOCK, BLOCK), 1)
    lower = column_index <= row_index
    difference = cumulative[:, :, :, None] - cumulative[:, :, None, :]
    decay = jnp.where(lower[None, None], jnp.exp(jnp.minimum(difference, 0.0)), 0.0)
    mixing = (scores[None] * decay * step_blocks[:, :, None, :]).astype(jnp.bfloat16)
    local_mix = jnp.einsum(
        "hkts,kshp->kthp", mixing, value_blocks, preferred_element_type=jnp.float32
    )
    weights = jnp.exp(block_ends[:, :, None] - cumulative) * step_blocks
    key_decayed = (write_blocks[None] * weights[:, None]).astype(jnp.bfloat16)
    increments = jnp.einsum(
        "hnks,kshp->khnp", key_decayed, value_blocks, preferred_element_type=jnp.float32
    )
    zero_state = jnp.zeros((head_count, state_count, head_width), jnp.float32)
    final, entering = lax.scan(block_chain, zero_state, (jnp.exp(block_ends).T, increments))
    return (local_mix, cumulative, block_ends, entering, final)


def mixer_finish(
    local_mix, cumulative, block_ends, entering, state_before, read_map, seq_inputs, skip_gain
):
    head_count = block_ends.shape[0]
    block_count = block_ends.shape[1]
    state_count = read_map.shape[0]
    head_width = entering.shape[3]
    before = jnp.cumsum(block_ends, axis=1) - block_ends
    states = jnp.exp(before).T[:, :, None, None] * state_before[None] + entering
    read_blocks = read_map.reshape(state_count, block_count, BLOCK).astype(jnp.float32)
    carried = jnp.einsum("nkt,khnp->kthp", read_blocks, states, precision=HIGHEST)
    carried = carried * jnp.exp(cumulative).transpose(1, 2, 0)[:, :, :, None]
    value_blocks = seq_inputs.reshape(block_count, BLOCK, head_count, head_width).astype(
        jnp.float32
    )
    output = local_mix + carried + skip_gain[None, None, :, None] * value_blocks
    return output.reshape(seq_inputs.shape).astype(jnp.bfloat16)


def expert_block(moe_tokens, expert_ids, route_weights, gate_proj, up_proj, down_proj):
    group_size = moe_tokens.shape[0]
    model_width = moe_tokens.shape[1]
    expert_count = lax.axis_size("exp") // 2
    capacity = min(group_size, 4 * group_size // expert_count)
    slot_count = expert_count * capacity
    assigned = expert_ids.reshape(group_size * 2)
    onehot = (
        assigned[:, None] == lax.broadcasted_iota(jnp.int32, (group_size * 2, expert_count), 1)
    ).astype(jnp.int32)
    earlier_count = jnp.cumsum(onehot, axis=0) - onehot
    position = jnp.sum((earlier_count + assigned[:, None] * capacity) * onehot, axis=1)
    matches = (
        position[:, None] == lax.broadcasted_iota(jnp.int32, (group_size * 2, slot_count), 1)
    ).astype(jnp.float32)
    dispatch = jnp.sum(matches.reshape(group_size, 2, slot_count), axis=1).astype(jnp.bfloat16)
    combine = jnp.sum(
        (matches * route_weights.reshape(group_size * 2)[:, None]).reshape(
            group_size, 2, slot_count
        ),
        axis=1,
    )
    gate_weight = gate_proj[0]
    up_weight = up_proj[0]
    down_weight = down_proj[0]
    packed = jnp.einsum(
        "is,id->sd", dispatch, moe_tokens, preferred_element_type=jnp.float32
    ).astype(jnp.bfloat16)
    doubled = jnp.broadcast_to(
        packed.reshape(expert_count, 1, capacity, model_width),
        (expert_count, 2, capacity, model_width),
    )
    arrived = lax.all_to_all(
        doubled.reshape(2 * slot_count, model_width), "exp", split_axis=0, concat_axis=0, tiled=True
    )
    gate_sums = jnp.dot(arrived, gate_weight, preferred_element_type=jnp.float32)
    up_sums = jnp.dot(arrived, up_weight, preferred_element_type=jnp.float32)
    hidden = (jax.nn.silu(gate_sums) * up_sums).astype(jnp.bfloat16)
    partial_out = jnp.dot(
        lax.all_gather(hidden, "ctx", axis=1, tiled=True),
        down_weight,
        preferred_element_type=jnp.float32,
    )
    returned = lax.all_to_all(partial_out, "exp", split_axis=0, concat_axis=0, tiled=True)
    summed = jnp.sum(returned.reshape(expert_count, 2, capacity, -1), axis=1).reshape(
        slot_count, -1
    )
    result = jnp.dot(combine, summed, precision=HIGHEST, preferred_element_type=jnp.float32)
    return result.astype(jnp.bfloat16)


MESH = pl.DeviceIdType.MESH
VMEM_BYTES = 60 * 2**20
GRID = 2
PAIR = 2


def expert_kernel(
    lines,
    tok_in,
    share,
    packed,
    gate_hbm,
    up_hbm,
    down_hbm,
    out,
    gathered,
    gate_w,
    up_w,
    down_w,
    tok,
    hid,
    acc,
    swap,
    ret,
    far_w,
    acc2,
    swap2,
    ret2,
    edge_in,
    states,
    load_sem,
    tsend,
    trecv,
    hsend_r,
    hsend_l,
    hrecv_l,
    hrecv_r,
    xsend,
    xrecv,
    rsend,
    rrecv,
    ssend,
    srecv,
    wsend,
    wrecv,
    x2send,
    x2recv,
    r2send,
    r2recv,
    esend,
    erecv,
):
    chunks = GRID * GRID
    z = lax.axis_index("ctx")
    e = lax.axis_index("exp")
    half = lax.rem(e, PAIR)
    other = 1 - half
    px = lax.rem(e // PAIR, GRID)
    py = e // (PAIR * GRID)
    rows = tok_in.shape[0]
    sub = rows // 2

    def peer(c, core):
        qx = lax.rem(px + lax.rem(c, GRID), GRID)
        qy = lax.rem(py + c // GRID, GRID)
        return (z, (qy * GRID + qx) * PAIR + core)

    mine = pl.ds(pl.multiple_of(half * rows, rows), rows)
    theirs = pl.ds(pl.multiple_of(other * rows, rows), rows)
    partner = (z, (py * GRID + px) * PAIR + other)

    loads = [
        pltpu.make_async_copy(gate_hbm, gate_w, load_sem.at[0]),
        pltpu.make_async_copy(up_hbm, up_w, load_sem.at[1]),
        pltpu.make_async_copy(tok_in, tok.at[0, mine], load_sem.at[3]),
        pltpu.make_async_copy(down_hbm, down_w, load_sem.at[2]),
    ]
    for load in loads[:3]:
        load.start()

    barrier = pltpu.get_barrier_semaphore()
    for device in (partner, peer(1, half), peer(2, half), peer(3, half)):
        pl.semaphore_signal(barrier, inc=1, device_id=device, device_id_type=MESH)

    for j in range(lines):

        @pl.when(z != j)
        def _():
            pl.semaphore_signal(barrier, inc=1, device_id=(j, e), device_id_type=MESH)

    pl.semaphore_wait(barrier, 4 + lines - 1)

    def remote(src, dst, ssem, rsem, device):
        return pltpu.make_async_remote_copy(
            src_ref=src,
            dst_ref=dst,
            send_sem=ssem,
            recv_sem=rsem,
            device_id=device,
            device_id_type=MESH,
        )

    upper = pl.ds(pl.multiple_of(half * rows, rows), sub)
    lower = pl.ds(pl.multiple_of(half * rows + sub, sub), sub)
    copies = [
        remote(tok_in, tok.at[0, mine], tsend.at[0], trecv.at[0], partner),
        remote(tok_in, tok.at[1, mine], tsend.at[1], trecv.at[1], peer(1, half)),
        remote(tok_in, tok.at[2, mine], tsend.at[2], trecv.at[2], peer(2, half)),
        remote(
            tok.at[1, upper], tok.at[3, upper], tsend.at[3], trecv.at[3], peer(2, half)
        ),
        remote(
            tok.at[2, lower], tok.at[3, lower], tsend.at[4], trecv.at[4], peer(1, half)
        ),
        remote(tok.at[1, mine], tok.at[1, mine], tsend.at[5], trecv.at[5], partner),
        remote(tok.at[2, mine], tok.at[2, mine], tsend.at[6], trecv.at[6], partner),
        remote(tok.at[3, mine], tok.at[3, mine], tsend.at[7], trecv.at[7], partner),
    ]
    for copy in copies[:3]:
        copy.start()

    last = chunks - 1
    assist = lines > 3
    edge = (z == 0) | (z == lines - 1)
    helper = (z == 1) | (z == lines - 2)
    far = jnp.where(z < 2, lines - 1, 0)
    piece = far_w.shape[0] // chunks

    def lend(k):
        span = pl.ds(k * piece, piece)
        target = jnp.where(z == 0, 1, lines - 2)
        return remote(
            down_hbm.at[far, span], far_w.at[span], wsend.at[k], wrecv.at[k], (target, e)
        )

    def start_lend(k):
        if assist:

            @pl.when(edge)
            def _():
                lend(k).start()

    def state_copy(j):
        return remote(packed, states.at[z], ssend.at[j], srecv.at[z], (j, e))

    start_lend(0)
    for j in range(lines):

        @pl.when(z != j)
        def _():
            state_copy(j).start()

    states[z] = packed[...]

    def make_hidden(c):
        width = gate_w.shape[1]
        x = tok[c]
        g = jnp.dot(x, gate_w[...], preferred_element_type=jnp.float32)
        u = jnp.dot(x, up_w[...], preferred_element_type=jnp.float32)
        hid[z, c] = (jax.nn.silu(g) * u).astype(jnp.bfloat16)

    def to_right(d, c):
        j = z - d
        return remote(hid.at[j, c], hid.at[j, c], hsend_r.at[d, c], hrecv_l.at[d, c], (z + 1, e))

    def to_left(d, c):
        j = z + d
        return remote(hid.at[j, c], hid.at[j, c], hsend_l.at[d, c], hrecv_r.at[d, c], (z - 1, e))

    def from_left(d, c):
        return remote(
            hid.at[z - d, c], hid.at[z - d, c], hsend_r.at[d, c], hrecv_l.at[d - 1, c], (z - 1, e)
        )

    def from_right(d, c):
        return remote(
            hid.at[z + d, c], hid.at[z + d, c], hsend_l.at[d, c], hrecv_r.at[d - 1, c], (z + 1, e)
        )

    def send_own(c):
        @pl.when(z < lines - 1)
        def _():
            to_right(0, c).start()

        @pl.when(z > 0)
        def _():
            to_left(0, c).start()

    def needed(d, c):
        return (c == last) if assist and d == lines - 1 else True

    def pass_on(d, c):
        @pl.when((z >= d) & needed(d, c))
        def _():
            from_left(d, c).wait_recv()

            @pl.when((z < lines - 1) & needed(d + 1, c))
            def _():
                to_right(d, c).start()

        @pl.when((z + d < lines) & needed(d, c))
        def _():
            from_right(d, c).wait_recv()

            @pl.when((z > 0) & needed(d + 1, c))
            def _():
                to_left(d, c).start()

    def add_down(j, c):
        acc[c] += jnp.dot(hid[j, c], down_w[j], preferred_element_type=jnp.float32)

    def add_both(d, c):
        @pl.when((z >= d) & needed(d, c))
        def _():
            add_down(z - d, c)

        @pl.when((z + d < lines) & needed(d, c))
        def _():
            add_down(z + d, c)

    def exchange(total, landing, ssem, rsem, c):
        return remote(total.at[c, theirs], landing.at[c], ssem.at[c], rsem.at[c], partner)

    def bring_home(total, landing, ssem, rsem, c):
        return remote(total.at[c, mine], landing.at[c], ssem.at[c], rsem.at[c], peer(c, half))

    def end_copy():
        target = jnp.where(z == 1, 0, lines - 1)
        return remote(acc2.at[0, mine], edge_in, esend.at[0], erecv.at[0], (target, e))

    loads[2].wait()
    loads[0].wait()
    loads[1].wait()
    loads[3].start()
    copies[0].wait_recv()
    make_hidden(0)
    send_own(0)
    start_lend(1)
    loads[3].wait()

    def chunk(c, carry):
        acc[c] = jnp.dot(hid[z, c], down_w[z], preferred_element_type=jnp.float32)
        pass_on(1, c)

        @pl.when(c == 0)
        def _():
            copies[1].wait_recv()
            copies[5].start()
            copies[3].start()
            copies[2].wait_recv()
            copies[6].start()
            copies[4].start()
            copies[5].wait_recv()

        @pl.when(c == 1)
        def _():
            copies[3].wait_recv()
            copies[4].wait_recv()
            copies[7].start()
            copies[6].wait_recv()

        @pl.when(c == 2)
        def _():
            copies[7].wait_recv()

        @pl.when(c < chunks - 1)
        def _():
            make_hidden(c + 1)

        if assist:

            @pl.when(helper & (c == last))
            def _():
                for k in range(chunks):
                    lend(k).wait_recv()
                for k in range(last):
                    acc2[k] = jnp.dot(
                        hid[far, k], far_w[...], preferred_element_type=jnp.float32
                    )
                    exchange(acc2, swap2, x2send, x2recv, k).start()
                for k in range(1, last):
                    exchange(acc2, swap2, x2send, x2recv, k).wait_recv()
                    acc2[k, mine] += swap2[k]
                    bring_home(acc2, ret2, r2send, r2recv, k).start()
                exchange(acc2, swap2, x2send, x2recv, 0).wait_recv()
                acc2[0, mine] = share[:, 0:1] * (acc2[0, mine] + swap2[0])

        for d in range(2, lines):
            pass_on(d, c)
            if d == 2:

                @pl.when(c < chunks - 1)
                def _():
                    send_own(c + 1)

                for k in range(2, chunks):

                    @pl.when(c == k - 2)
                    def _():
                        start_lend(k)

            add_both(d - 1, c)
        add_both(lines - 1, c)

        exchange(acc, swap, xsend, xrecv, c).start()
        exchange(acc, swap, xsend, xrecv, c).wait_recv()
        acc[c, mine] += swap[c]

        @pl.when(c > 0)
        def _():
            bring_home(acc, ret, rsend, rrecv, c).start()

        if assist:

            @pl.when(helper & (c == last))
            def _():
                for k in range(1, last):
                    bring_home(acc2, ret2, r2send, r2recv, k).wait_recv()
                    acc2[0, mine] += share[:, k : k + 1] * ret2[k]
                end_copy().start()

        return carry

    lax.fori_loop(0, chunks, chunk, 0)

    for j in range(lines):

        @pl.when(z != j)
        def _():
            remote(packed, states.at[j], ssend.at[j], srecv.at[j], (j, e)).wait_recv()

    gathered[...] = states[...]
    total = share[:, 0:1] * acc[0, mine]
    for c in range(1, chunks):
        bring_home(acc, ret, rsend, rrecv, c).wait_recv()
        total += share[:, c : c + 1] * ret[c]
    swap[0] = total
    if assist:

        @pl.when(edge)
        def _():
            end_copy().wait_recv()
            swap[0] += edge_in[...]

    out[...] = swap[0].astype(out.dtype)

    for j in range(lines):

        @pl.when(z != j)
        def _():
            state_copy(j).wait_send()

    if assist:

        @pl.when(edge)
        def _():
            for k in range(chunks):
                lend(k).wait_send()

        @pl.when(helper)
        def _():
            for k in range(last):
                exchange(acc2, swap2, x2send, x2recv, k).wait_send()
                if k > 0:
                    bring_home(acc2, ret2, r2send, r2recv, k).wait_send()
            end_copy().wait_send()

    for copy in copies:
        copy.wait_send()
    for c in range(chunks):
        for d in range(lines - 1):
            if assist and d == lines - 2 and c < last:
                continue

            @pl.when((z >= d) & (z < lines - 1))
            def _():
                to_right(d, c).wait_send()

            @pl.when((z + d < lines) & (z > 0))
            def _():
                to_left(d, c).wait_send()

        exchange(acc, swap, xsend, xrecv, c).wait_send()
        if c > 0:
            bring_home(acc, ret, rsend, rrecv, c).wait_send()


def expert_fused(packed, moe_tokens, expert_ids, route_weights, gate_proj, up_proj, down_proj):
    lines = lax.axis_size("ctx")
    chunks = GRID * GRID
    rows, width = moe_tokens.shape
    part = gate_proj.shape[2]
    columns = down_proj.shape[2]
    place = lax.axis_index("exp") // PAIR
    px, py = place % GRID, place // GRID
    order = jnp.stack(
        [((py + c // GRID) % GRID) * GRID + (px + c % GRID) % GRID for c in range(chunks)]
    )
    share = jnp.sum(
        jnp.where(expert_ids[:, :, None] == order[None, None, :], route_weights[:, :, None], 0.0),
        axis=1,
    )
    f32, bf16 = jnp.float32, jnp.bfloat16
    dma = pltpu.SemaphoreType.DMA
    vmem = pl.BlockSpec(memory_space=pltpu.VMEM)
    hbm = pl.BlockSpec(memory_space=pl.ANY)
    return pl.pallas_call(
        functools.partial(expert_kernel, lines),
        out_shape=(
            jax.ShapeDtypeStruct((rows, columns), bf16),
            jax.ShapeDtypeStruct((lines, *packed.shape), f32),
        ),
        in_specs=[vmem, vmem, vmem, hbm, hbm, hbm],
        out_specs=(vmem, vmem),
        scratch_shapes=[
            pltpu.VMEM((width, part), bf16),
            pltpu.VMEM((width, part), bf16),
            pltpu.VMEM((lines, part, columns), bf16),
            pltpu.VMEM((chunks, PAIR * rows, width), bf16),
            pltpu.VMEM((lines, chunks, PAIR * rows, part), bf16),
            pltpu.VMEM((chunks, PAIR * rows, columns), f32),
            pltpu.VMEM((chunks, rows, columns), f32),
            pltpu.VMEM((chunks, rows, columns), f32),
            pltpu.VMEM((part, columns), bf16),
            pltpu.VMEM((chunks - 1, PAIR * rows, columns), f32),
            pltpu.VMEM((chunks - 1, rows, columns), f32),
            pltpu.VMEM((chunks - 1, rows, columns), f32),
            pltpu.VMEM((rows, columns), f32),
            pltpu.VMEM((lines, *packed.shape), f32),
            dma((4,)),
            dma((8,)),
            dma((8,)),
            dma((lines, chunks)),
            dma((lines, chunks)),
            dma((lines, chunks)),
            dma((lines, chunks)),
            dma((chunks,)),
            dma((chunks,)),
            dma((chunks,)),
            dma((chunks,)),
            dma((lines,)),
            dma((lines,)),
            dma((chunks,)),
            dma((chunks,)),
            dma((chunks,)),
            dma((chunks,)),
            dma((chunks,)),
            dma((chunks,)),
            dma((1,)),
            dma((1,)),
        ],
        compiler_params=pltpu.CompilerParams(
            collective_id=0, has_side_effects=True, vmem_limit_bytes=VMEM_BYTES
        ),
    )(
        moe_tokens,
        share,
        packed,
        gate_proj[0],
        up_proj[0],
        down_proj[0].reshape(lines, part, columns),
    )


def expert_layer(packed, *arrays):
    moe_tokens, gate_proj, down_proj = arrays[0], arrays[3], arrays[5]
    if lax.axis_size("exp") == PAIR * GRID * GRID and gate_proj.shape[2] % 128 == 0:
        return expert_fused(packed, *arrays)
    return expert_block(*arrays), lax.all_gather(packed, "ctx")


def on_device(
    seq_inputs,
    step_size,
    write_map,
    read_map,
    decay_log,
    skip_gain,
    moe_tokens,
    expert_ids,
    route_weights,
    gate_proj,
    up_proj,
    down_proj,
):
    local_mix, cumulative, block_ends, entering, final = mixer_prepare(
        seq_inputs, step_size, write_map, read_map, decay_log
    )
    total_log = jnp.sum(block_ends, axis=1)
    head_count, state_count, head_width = final.shape
    logs = jnp.broadcast_to(total_log[:, None, None], (head_count, 8, head_width))
    packed = jnp.concatenate([final, logs], axis=1)
    expert_output, gathered = expert_layer(
        packed, moe_tokens, expert_ids, route_weights, gate_proj, up_proj, down_proj
    )
    place = lax.axis_index("ctx")
    state_before = jnp.zeros_like(final)
    for lap in range(lax.axis_size("ctx")):
        latter = gathered[lap]
        decay = jnp.exp(latter[:, state_count, 0])
        added = decay[:, None, None] * state_before + latter[:, :state_count]
        state_before = jnp.where(lap < place, added, state_before)
    mixer_output = mixer_finish(
        local_mix, cumulative, block_ends, entering, state_before, read_map, seq_inputs, skip_gain
    )
    return (mixer_output, expert_output)


def solution(mesh):
    return jax.shard_map(
        on_device,
        mesh=mesh,
        in_specs=(
            P("ctx", "exp"),
            P("exp", "ctx"),
            P(None, "ctx"),
            P(None, "ctx"),
            P("exp"),
            P("exp"),
            P("exp", None),
            P("exp", None),
            P("exp", None),
            P("exp", None, "ctx"),
            P("exp", None, "ctx"),
            P("exp", None, "ctx"),
        ),
        out_specs=(P("ctx", "exp"), P("exp", "ctx")),
        check_vma=False,
    )
```

profile of v0, /device:TPU:0, one launch (start us, length us, event | category | flops | bytes accessed | tf_op | source)
XLA Modules:
  0.0 154.7 jit_solution(15490420588411281998)
XLA Ops:
  0.7 0.1 pad_add_fusion
  0.8 0.7 exponential_negate_fusion
  1.5 0.8 select_reduce_fusion
  2.2 0.8 broadcast_multiply_fusion
  3.0 0.2 fusion.12
  3.2 0.2 slice_reduce_fusion
  3.5 0.8 exponential_multiply_fusion
  4.3 0.1 broadcast_in_dim.35
  4.3 0.7 reshape.54
  5.1 0.7 reshape.53
  5.8 0.7 copy.37.share
  6.6 1.2 reshape.60
  7.8 0.3 copy.34
  8.1 0.2 fusion.14
  8.2 0.2 while.13
  8.3 0.1 bitcast_add_fusion.2
  8.4 0.1 bitcast_add_fusion.2
  8.5 0.6 pad_maximum_fusion.packed
  9.1 0.0 copy-start.1
  9.1 0.0 copy-start.2
  9.1 0.0 copy-start.3
  9.1 0.0 copy-start.4
  9.1 140.5 %shard_map.131 = (bf16[128,1024]{1,0:T(8,128)(2,1)}, f32[4,4,24,64]{3,2,1,0:T(8,128)}) custom-call(bf16[128,4096]{1,0:T(8,128)(2,1)} %tok_in.1, f32[128,4]{1,0:T(8,128)} %copy.37.share, f32[4,24,64]{2,1,0:T(8,128)} %pad_maximum_fusion.packed, bf16[4096,896]{1,0:T(8,128)(2,1)} %bitcast.62, bf16[4096,896]{1,0:T(8,128)(2,1)} %bitcast.63, ...), custom_call_target="tpu_custom_call" | custom-call | tf_op jit(solution)/shard_map/pallas_call | solution.py:535
  149.6 0.9 slice_bitcast_fusion
  150.5 0.1 fusion.34
  150.7 0.1 fusion.32
  150.8 0.1 fusion.19
  150.9 0.6 fusion.1
  151.4 0.0 copy-done.1
  151.5 0.0 copy-done.2
  151.5 0.3 fusion.25
  151.7 0.0 copy-done.3
  151.7 0.0 copy-done.4
  151.8 0.0 copy-start
  151.8 0.8 fusion.4
  152.6 0.3 copy.45
  152.9 1.0 reshape.59
  153.9 0.0 copy-done
  153.9 0.7 copy.72
  (10 shorter events, 0.1 us)
Async XLA Ops:
  9.1 142.4 %copy-start.1 = (bf16[16,512]{1,0:T(8,128)(2,1)S(1)}, bf16[16,512]{1,0:T(8,128)(2,1)}, u32[]{:S(2)}) copy-start(bf16[16,512]{1,0:T(8,128)(2,1)} %param.16) | copy-start | bytes 49156
  9.1 142.4 %copy-start.2 = (bf16[16,512]{1,0:T(8,128)(2,1)S(1)}, bf16[16,512]{1,0:T(8,128)(2,1)}, u32[]{:S(2)}) copy-start(bf16[16,512]{1,0:T(8,128)(2,1)} %param.17) | copy-start | bytes 49156
  9.1 142.6 %copy-start.3 = (f32[4,512]{1,0:T(4,128)S(1)}, f32[4,512]{1,0:T(4,128)}, u32[]{:S(2)}) copy-start(f32[4,512]{1,0:T(4,128)} %param.15) | copy-start | bytes 24580
  9.1 142.7 %copy-start.4 = (f32[4]{0:T(128)S(1)}, f32[4]{0:T(128)}, u32[]{:S(2)}) copy-start(f32[4]{0:T(128)} %param.19) | copy-start | bytes 52
  151.8 2.2 %copy-start = (bf16[128,1024]{1,0:T(8,128)(2,1)S(1)}, bf16[128,1024]{1,0:T(8,128)(2,1)}, u32[]{:S(2)}) copy-start(bf16[128,1024]{1,0:T(8,128)(2,1)} %get-tuple-element.137) | copy-start | bytes 786436
where the time goes:
time: 155 us
  Pallas kernels  141 us (91%)
  local copies, waits for them, and re-layouts  6.84 us (4%)
  other arithmetic  4.38 us (3%)
  matrix products  2 us (1%)
    pallas_call x1, Pallas kernels, expert_fused(): pl.pallas_call(functools.partial(expert_kernel, lines), out_shape=(jax.Sh...  141 us

commit v1 on v0

v1 whole, which is shorter than its diff:
```python
import jax
import jax.numpy as jnp
from jax import lax
from jax.experimental import pallas as pl
from jax.experimental.pallas import tpu as pltpu
from jax.sharding import PartitionSpec as P

BLOCK = 256


HIGHEST = lax.Precision.HIGHEST


def block_chain(running, pieces):
    decay, increment = pieces
    return (decay[:, None, None] * running + increment, running)


def mixer_prepare(seq_inputs, step_size, write_map, read_map, decay_log):
    length = seq_inputs.shape[0]
    head_count = step_size.shape[0]
    state_count = write_map.shape[0]
    head_width = seq_inputs.shape[1] // head_count
    block_count = length // BLOCK
    decay_rate = -jnp.exp(decay_log)
    log_decay = (step_size * decay_rate[:, None]).reshape(head_count, block_count, BLOCK)
    order = lax.broadcasted_iota(jnp.int32, (BLOCK, BLOCK), 0)
    until = (order <= lax.broadcasted_iota(jnp.int32, (BLOCK, BLOCK), 1)).astype(jnp.float32)
    cumulative = jnp.einsum("hks,st->hkt", log_decay, until, precision=HIGHEST)
    block_ends = cumulative[:, :, BLOCK - 1]
    step_blocks = step_size.reshape(head_count, block_count, BLOCK)
    write_blocks = write_map.reshape(state_count, block_count, BLOCK)
    read_blocks = read_map.reshape(state_count, block_count, BLOCK)
    value_blocks = seq_inputs.reshape(block_count, BLOCK, head_count, head_width)
    scores = jnp.einsum(
        "nkt,nks->kts", read_blocks, write_blocks, preferred_element_type=jnp.float32
    )
    row_index = lax.broadcasted_iota(jnp.int32, (BLOCK, BLOCK), 0)
    column_index = lax.broadcasted_iota(jnp.int32, (BLOCK, BLOCK), 1)
    lower = column_index <= row_index
    difference = cumulative[:, :, :, None] - cumulative[:, :, None, :]
    decay = jnp.where(lower[None, None], jnp.exp(jnp.minimum(difference, 0.0)), 0.0)
    mixing = (scores[None] * decay * step_blocks[:, :, None, :]).astype(jnp.bfloat16)
    local_mix = jnp.einsum(
        "hkts,kshp->kthp", mixing, value_blocks, preferred_element_type=jnp.float32
    )
    weights = jnp.exp(block_ends[:, :, None] - cumulative) * step_blocks
    key_decayed = (write_blocks[None] * weights[:, None]).astype(jnp.bfloat16)
    increments = jnp.einsum(
        "hnks,kshp->khnp", key_decayed, value_blocks, preferred_element_type=jnp.float32
    )
    zero_state = jnp.zeros((head_count, state_count, head_width), jnp.float32)
    final, entering = lax.scan(block_chain, zero_state, (jnp.exp(block_ends).T, increments))
    return (local_mix, cumulative, block_ends, entering, final)


def mixer_finish(
    local_mix, cumulative, block_ends, entering, state_before, read_map, seq_inputs, skip_gain
):
    head_count = block_ends.shape[0]
    block_count = block_ends.shape[1]
    state_count = read_map.shape[0]
    head_width = entering.shape[3]
    before = jnp.cumsum(block_ends, axis=1) - block_ends
    states = jnp.exp(before).T[:, :, None, None] * state_before[None] + entering
    read_blocks = read_map.reshape(state_count, block_count, BLOCK).astype(jnp.float32)
    carried = jnp.einsum("nkt,khnp->kthp", read_blocks, states, precision=HIGHEST)
    carried = carried * jnp.exp(cumulative).transpose(1, 2, 0)[:, :, :, None]
    value_blocks = seq_inputs.reshape(block_count, BLOCK, head_count, head_width).astype(
        jnp.float32
    )
    output = local_mix + carried + skip_gain[None, None, :, None] * value_blocks
    return output.reshape(seq_inputs.shape).astype(jnp.bfloat16)


def expert_block(moe_tokens, expert_ids, route_weights, gate_proj, up_proj, down_proj):
    group_size = moe_tokens.shape[0]
    model_width = moe_tokens.shape[1]
    expert_count = lax.axis_size("exp") // 2
    capacity = min(group_size, 4 * group_size // expert_count)
    slot_count = expert_count * capacity
    assigned = expert_ids.reshape(group_size * 2)
    onehot = (
        assigned[:, None] == lax.broadcasted_iota(jnp.int32, (group_size * 2, expert_count), 1)
    ).astype(jnp.int32)
    earlier_count = jnp.cumsum(onehot, axis=0) - onehot
    position = jnp.sum((earlier_count + assigned[:, None] * capacity) * onehot, axis=1)
    matches = (
        position[:, None] == lax.broadcasted_iota(jnp.int32, (group_size * 2, slot_count), 1)
    ).astype(jnp.float32)
    dispatch = jnp.sum(matches.reshape(group_size, 2, slot_count), axis=1).astype(jnp.bfloat16)
    combine = jnp.sum(
        (matches * route_weights.reshape(group_size * 2)[:, None]).reshape(
            group_size, 2, slot_count
        ),
        axis=1,
    )
    gate_weight = gate_proj[0]
    up_weight = up_proj[0]
    down_weight = down_proj[0]
    packed = jnp.einsum(
        "is,id->sd", dispatch, moe_tokens, preferred_element_type=jnp.float32
    ).astype(jnp.bfloat16)
    doubled = jnp.broadcast_to(
        packed.reshape(expert_count, 1, capacity, model_width),
        (expert_count, 2, capacity, model_width),
    )
    arrived = lax.all_to_all(
        doubled.reshape(2 * slot_count, model_width), "exp", split_axis=0, concat_axis=0, tiled=True
    )
    gate_sums = jnp.dot(arrived, gate_weight, preferred_element_type=jnp.float32)
    up_sums = jnp.dot(arrived, up_weight, preferred_element_type=jnp.float32)
    hidden = (jax.nn.silu(gate_sums) * up_sums).astype(jnp.bfloat16)
    partial_out = jnp.dot(
        lax.all_gather(hidden, "ctx", axis=1, tiled=True),
        down_weight,
        preferred_element_type=jnp.float32,
    )
    returned = lax.all_to_all(partial_out, "exp", split_axis=0, concat_axis=0, tiled=True)
    summed = jnp.sum(returned.reshape(expert_count, 2, capacity, -1), axis=1).reshape(
        slot_count, -1
    )
    result = jnp.dot(combine, summed, precision=HIGHEST, preferred_element_type=jnp.float32)
    return result.astype(jnp.bfloat16)


MESH = pl.DeviceIdType.MESH
VMEM_BYTES = 61 * 2**20
GRID = 2
PAIR = 2
LINES = 4
CHUNKS = GRID * GRID
UNITS = 2 * CHUNKS
GROUPS = 4
F32 = jnp.float32
BF16 = jnp.bfloat16


def unit_of(t):
    return jnp.where(t == 3, 4, jnp.where(t == 4, 3, t))


def fused_kernel(
    tok_hbm,
    ids_hbm,
    route_hbm,
    seq_hbm,
    step_hbm,
    write_hbm,
    read_hbm,
    decay_ref,
    skip_ref,
    gate_hbm,
    up_hbm,
    down_hbm,
    mix_out,
    out,
    gate_w,
    up_w,
    down_w,
    tok,
    hid,
    acc,
    swap,
    ret,
    far_w,
    acc2,
    swap2,
    ret2,
    rsum,
    edge_in,
    ids,
    route,
    seq,
    step,
    write,
    read,
    local,
    grown,
    entering,
    before,
    packed,
    states,
    load_sem,
    small_sem,
    tsend,
    trecv,
    own_in_send,
    own_out_send,
    fwd_in_send,
    fwd_out_send,
    hrecv,
    wsend,
    wrecv,
    rsend,
    rrecv,
    xsend,
    xrecv,
    bsend,
    brecv,
    x2send,
    x2recv,
    b2send,
    b2recv,
    ssend,
    srecv,
):
    z = lax.axis_index("ctx")
    e = lax.axis_index("exp")
    half = lax.rem(e, PAIR)
    other = 1 - half
    px = lax.rem(e // PAIR, GRID)
    py = e // (PAIR * GRID)
    sub = tok.shape[1] // 2
    quarter = sub // 2
    part = gate_w.shape[1]
    first = part // 256 * 128
    columns = acc.shape[2]
    wide = columns // GROUPS

    end = (z == 0) | (z == LINES - 1)
    inside = (z > 0) & (z < LINES - 1)
    low = z < 2
    inner = jnp.where(low, z + 1, z - 1)
    outer = jnp.where(low, z - 1, z + 1)
    near = jnp.where(end, inner, outer)
    far = jnp.where(end, LINES - 1 - inner, inner)
    opposite = jnp.where(low, LINES - 1, 0)

    def peer(c, core):
        qx = lax.rem(px + c % GRID, GRID)
        qy = lax.rem(py + c // GRID, GRID)
        return (z, (qy * GRID + qx) * PAIR + core)

    partner = peer(0, other)
    mine = pl.ds(pl.multiple_of(half * sub, sub), sub)
    theirs = pl.ds(pl.multiple_of(other * sub, sub), sub)
    mine_a = pl.ds(pl.multiple_of(half * sub, quarter), quarter)
    mine_b = pl.ds(pl.multiple_of(half * sub + quarter, quarter), quarter)

    def remote(src, dst, ssem, rsem, device):
        return pltpu.make_async_remote_copy(
            src_ref=src,
            dst_ref=dst,
            send_sem=ssem,
            recv_sem=rsem,
            device_id=device,
            device_id_type=MESH,
        )

    left, right = pl.ds(0, first), pl.ds(first, part - first)
    loads = [
        pltpu.make_async_copy(tok_hbm.at[pl.ds(0, sub)], tok.at[0, mine], load_sem.at[0]),
        pltpu.make_async_copy(gate_hbm.at[:, left], gate_w.at[:, left], load_sem.at[1]),
        pltpu.make_async_copy(up_hbm.at[:, left], up_w.at[:, left], load_sem.at[2]),
        pltpu.make_async_copy(gate_hbm.at[:, right], gate_w.at[:, right], load_sem.at[3]),
        pltpu.make_async_copy(up_hbm.at[:, right], up_w.at[:, right], load_sem.at[4]),
        pltpu.make_async_copy(tok_hbm.at[pl.ds(sub, sub)], tok.at[1, mine], load_sem.at[5]),
        pltpu.make_async_copy(down_hbm, down_w, load_sem.at[6]),
    ]
    small = [
        pltpu.make_async_copy(src, dst, small_sem.at[i])
        for i, (src, dst) in enumerate(
            [
                (step_hbm, step),
                (write_hbm, write),
                (read_hbm, read),
                (seq_hbm, seq),
                (ids_hbm, ids),
                (route_hbm, route),
            ]
        )
    ]
    for load in loads[:6]:
        load.start()
    for load in small:
        load.start()

    barrier = pltpu.get_barrier_semaphore()
    for device in (partner, peer(1, half), peer(2, half), peer(3, half)):
        pl.semaphore_signal(barrier, inc=1, device_id=device, device_id_type=MESH)
    for j in range(LINES):

        @pl.when(z != j)
        def _():
            pl.semaphore_signal(barrier, inc=1, device_id=(j, e), device_id_type=MESH)

    pl.semaphore_wait(barrier, 4 + LINES - 1)

    def tok_rows(h):
        return tok_hbm.at[pl.ds(h * sub, sub)]

    to_partner = [
        remote(tok_rows(h), tok.at[h, mine], tsend.at[h], trecv.at[h], partner) for h in range(2)
    ]
    to_x = [
        remote(tok_rows(h), tok.at[2 + h, mine], tsend.at[2 + h], trecv.at[2 + h], peer(1, half))
        for h in range(2)
    ]
    to_y = [
        remote(tok_rows(h), tok.at[4 + h, mine], tsend.at[4 + h], trecv.at[4 + h], peer(2, half))
        for h in range(2)
    ]
    pass_x = [
        remote(
            tok.at[4 + h, mine_a], tok.at[6 + h, mine_a], tsend.at[6 + h], trecv.at[6 + h],
            peer(1, half),
        )
        for h in range(2)
    ]
    pass_y = [
        remote(
            tok.at[2 + h, mine_b], tok.at[6 + h, mine_b], tsend.at[8 + h], trecv.at[8 + h],
            peer(2, half),
        )
        for h in range(2)
    ]
    across = {
        n: remote(tok.at[n, mine], tok.at[n, mine], tsend.at[8 + n], trecv.at[8 + n], partner)
        for n in range(2, UNITS)
    }
    for h in range(2):
        to_partner[h].start()
        to_x[h].start()
        to_y[h].start()

    def lend(k):
        if k < 2:
            span = pl.ds(k * (wide // 2), wide // 2)
        else:
            span = pl.ds((k - 1) * wide, wide)
        return remote(
            down_hbm.at[opposite, :, span], far_w.at[:, span], wsend.at[k], wrecv.at[k], (inner, e)
        )

    @pl.when(end)
    def _():
        lend(0).start()

    def own_in(n):
        kind = jnp.where(end, 0, 1)
        return remote(
            hid.at[z, n], hid.at[z, n], own_in_send.at[n], hrecv.at[kind, n], (inner, e)
        )

    def own_out(n):
        return remote(hid.at[z, n], hid.at[z, n], own_out_send.at[n], hrecv.at[0, n], (outer, e))

    def fwd_in(n):
        return remote(
            hid.at[near, n], hid.at[near, n], fwd_in_send.at[n], hrecv.at[2, n], (inner, e)
        )

    def fwd_out(n):
        return remote(
            hid.at[far, n], hid.at[far, n], fwd_out_send.at[n], hrecv.at[1, n], (outer, e)
        )

    def arrived(kind, j, n):
        remote(hid.at[j, n], hid.at[j, n], own_in_send.at[n], hrecv.at[kind, n], (near, e)).wait_recv()

    def state_copy(j):
        return remote(packed, states.at[z], ssend.at[j], srecv.at[z], (j, e))

    head_count = step.shape[0]
    length = step.shape[1]
    state_count = write.shape[0]
    lanes = seq.shape[1]
    block_count = length // BLOCK
    lane_head = lax.broadcasted_iota(jnp.int32, (1, lanes), 1) // (lanes // head_count)

    def mixer_first():
        for load in small[:4]:
            load.wait()
        rows = lax.broadcasted_iota(jnp.int32, (BLOCK, BLOCK), 0)
        cols = lax.broadcasted_iota(jnp.int32, (BLOCK, BLOCK), 1)
        lower = cols <= rows
        until = (rows <= cols).astype(F32)
        since = lower.astype(F32)
        head_row = lax.broadcasted_iota(jnp.int32, (head_count, 1), 0)
        rate = jnp.zeros((head_count, 1), F32)
        for h in range(head_count):
            rate = jnp.where(head_row == h, -jnp.exp(jnp.full((head_count, 1), decay_ref[h])), rate)
        state = jnp.zeros((state_count, lanes), F32)
        gone = jnp.zeros((1, lanes), F32)
        for k in range(block_count):
            span = pl.ds(k * BLOCK, BLOCK)
            steps = step[:, span]
            log_decay = steps * rate
            cumulative = jnp.dot(
                log_decay, until, precision=HIGHEST, preferred_element_type=F32
            )
            upright = lax.dot_general(
                since,
                log_decay,
                (((1,), (1,)), ((), ())),
                precision=HIGHEST,
                preferred_element_type=F32,
            )
            block_end = cumulative[:, BLOCK - 1 :]
            weights = jnp.exp(block_end - cumulative) * steps
            keys = write[:, span]
            scores = lax.dot_general(
                read[:, span], keys, (((0,), (0,)), ((), ())), preferred_element_type=F32
            )
            values = seq[span, :]
            mixed = jnp.zeros((BLOCK, lanes), F32)
            risen = jnp.zeros((BLOCK, lanes), F32)
            increment = jnp.zeros((state_count, lanes), F32)
            ends = jnp.zeros((1, lanes), F32)
            for h in range(head_count):
                here = lane_head == h
                difference = upright[:, h : h + 1] - cumulative[h : h + 1, :]
                decay = jnp.where(lower, jnp.exp(jnp.minimum(difference, 0.0)), 0.0)
                mixing = (scores * decay * steps[h : h + 1, :]).astype(BF16)
                mixed = jnp.where(
                    here, jnp.dot(mixing, values, preferred_element_type=F32), mixed
                )
                risen = jnp.where(here, upright[:, h : h + 1], risen)
                decayed = (keys.astype(F32) * weights[h : h + 1, :]).astype(BF16)
                increment = jnp.where(
                    here, jnp.dot(decayed, values, preferred_element_type=F32), increment
                )
                ends = jnp.where(here, block_end[h : h + 1, :], ends)
            local[span, :] = mixed
            grown[span, :] = jnp.exp(risen)
            entering[k] = state
            before[k] = jnp.broadcast_to(gone, (8, lanes))
            state = jnp.exp(ends) * state + increment
            gone = gone + ends
        packed[0:state_count, :] = state
        packed[state_count:, :] = jnp.broadcast_to(gone, (8, lanes))
        states[z] = packed[...]
        for j in range(LINES):

            @pl.when(z != j)
            def _():
                state_copy(j).start()

    def mixer_second():
        for j in range(LINES):

            @pl.when(z != j)
            def _():
                remote(packed, states.at[j], ssend.at[j], srecv.at[j], (j, e)).wait_recv()

        state = jnp.zeros((state_count, lanes), F32)
        for lap in range(LINES):
            latter = states[lap]
            added = jnp.exp(latter[state_count : state_count + 1, :]) * state + latter[:state_count, :]
            state = jnp.where(lap < z, added, state)
        gain = jnp.zeros((1, lanes), F32)
        for h in range(head_count):
            gain = jnp.where(lane_head == h, skip_ref[h], gain)
        for k in range(block_count):
            span = pl.ds(k * BLOCK, BLOCK)
            full = jnp.exp(before[k][0:1, :]) * state + entering[k]
            carried = lax.dot_general(
                read[:, span].astype(F32),
                full,
                (((0,), (0,)), ((), ())),
                precision=HIGHEST,
                preferred_element_type=F32,
            )
            total = local[span, :] + carried * grown[span, :] + gain * seq[span, :].astype(F32)
            mix_out[span, :] = total.astype(mix_out.dtype)

    def share(c, h):
        qx = lax.rem(px + c % GRID, GRID)
        qy = lax.rem(py + c // GRID, GRID)
        named = ids[h * sub : (h + 1) * sub, :] == qy * GRID + qx
        return jnp.sum(jnp.where(named, route[h * sub : (h + 1) * sub, :], 0.0), axis=1, keepdims=True)

    def add_down(j, n):
        acc[n] += jnp.dot(hid[j, n], down_w[j], preferred_element_type=F32)

    def make_hidden(n, span):
        x = tok[n]
        g = jnp.dot(x, gate_w[:, span], preferred_element_type=F32)
        u = jnp.dot(x, up_w[:, span], preferred_element_type=F32)
        hid[z, n, :, span] = (jax.nn.silu(g) * u).astype(BF16)

    def tokens_ready(t):
        if t < 2:
            loads[0 if t == 0 else 5].wait()
            to_partner[t].wait_recv()
        if t == 2 or t == 4:
            h = (t - 2) // 2
            to_x[h].wait_recv()
            across[2 + h].start()
            to_y[h].wait_recv()
            across[4 + h].start()
            pass_x[h].start()
            pass_y[h].start()
            across[2 + h].wait_recv()
        if t == 3 or t == 5:
            across[4 + (t - 3) // 2].wait_recv()
        if t >= 6:
            pass_x[t - 6].wait_recv()
            pass_y[t - 6].wait_recv()
            across[t].start()
            across[t].wait_recv()

    def take_far(n):
        arrived(1, far, n)

        @pl.when(inside)
        def _():
            fwd_out(n).start()

        add_down(far, n)

    def forward_step(t, carry):
        @pl.when(t < UNITS)
        def _():
            n = unit_of(t)
            for k in range(UNITS):

                @pl.when(t == k)
                def _():
                    if k == 2:
                        mixer_first()
                    tokens_ready(k)

            @pl.when(t == 0)
            def _():
                loads[1].wait()
                loads[2].wait()

            make_hidden(n, left)

            @pl.when(t == 0)
            def _():
                loads[3].wait()
                loads[4].wait()
                loads[6].start()

            make_hidden(n, right)

            @pl.when(inside)
            def _():
                own_out(n).start()

            @pl.when(end | (t < 2))
            def _():
                own_in(n).start()

            @pl.when(t == 0)
            def _():
                loads[6].wait()

            acc[n] = jnp.dot(hid[z, n], down_w[z], preferred_element_type=F32)

        @pl.when(t >= 2)
        def _():
            n = unit_of(t - 2)
            arrived(0, near, n)

            @pl.when(inside)
            def _():
                fwd_in(n).start()

            add_down(near, n)

        @pl.when(inside & (t > 3) & (t < 6))
        def _():
            take_far(t - 4)

        @pl.when(t == UNITS - 1)
        def _():
            @pl.when(inside)
            def _():
                own_in(2).start()
                own_in(4).start()

            @pl.when(end)
            def _():
                for k in range(1, GROUPS + 1):
                    lend(k).start()

        return carry

    lax.fori_loop(0, UNITS + 2, forward_step, 0)

    @pl.when(inside)
    def _():
        for n in (3, 5, 6, 7):
            own_in(n).start()

    def exchange(n):
        return remote(acc.at[n, theirs], swap.at[n], xsend.at[n], xrecv.at[n], partner)

    def bring_home(n):
        return remote(acc.at[n, mine], ret.at[n - 2], bsend.at[n], brecv.at[n], peer(n // 2, half))

    def finish(n):
        exchange(n).wait_recv()
        acc[n, mine] += swap[n]

    def send_home(n):
        for k in range(2, UNITS):

            @pl.when(n == k)
            def _():
                bring_home(k).start()

    def exchange2(k):
        return remote(acc2.at[k, :, theirs], swap2.at[k], x2send.at[k], x2recv.at[k], partner)

    def bring_home2(k, c):
        return remote(
            acc2.at[k, pl.ds(2 * c, 2), mine],
            ret2.at[k, c - 1],
            b2send.at[k, c],
            b2recv.at[k, c],
            peer(c, half),
        )

    def edge_copy(k):
        return remote(rsum.at[k], edge_in.at[k], rsend.at[k], rrecv.at[k], (outer, e))

    def helper_dot(k):
        @pl.when(k == 0)
        def _():
            lend(0).wait_recv()
            lend(1).wait_recv()

        for i in range(1, GROUPS):

            @pl.when(k == i)
            def _():
                lend(i + 1).wait_recv()

        span = pl.ds(pl.multiple_of(k * wide, wide), wide)

        def one(n, carry):
            acc2[k, n] = jnp.dot(hid[opposite, n], far_w[:, span], preferred_element_type=F32)
            return carry

        lax.fori_loop(0, UNITS, one, 0)
        exchange2(k).start()

    def helper_home(k):
        exchange2(k).wait_recv()
        acc2[k, :, mine] += swap2[k]
        for c in range(1, CHUNKS):
            bring_home2(k, c).start()

    def helper_edge(k):
        for c in range(1, CHUNKS):
            bring_home2(k, c).wait_recv()
        for h in range(2):
            total = share(0, h) * acc2[k, h, mine]
            for c in range(1, CHUNKS):
                total += share(c, h) * ret2[k, c - 1, h]
            rsum[k, pl.ds(h * sub, sub)] = total
        edge_copy(k).start()

    def finish_step(s, carry):
        @pl.when((end & (s < UNITS)) | ((s > 1) & (s < UNITS)))
        def _():
            take_far(unit_of(s))

        @pl.when(inside & (s > 1) & (s < 4))
        def _():
            def one(i, inner_carry):
                n = unit_of((s - 2) * 4 + i)
                arrived(2, opposite, n)
                add_down(opposite, n)
                return inner_carry

            lax.fori_loop(0, 4, one, 0)

        @pl.when(s == 3)
        def _():
            for k in range(4):
                exchange(k if k < 3 else 4).start()

        @pl.when((s > 3) & (s < UNITS))
        def _():
            exchange(unit_of(s)).start()

        @pl.when(s == 4)
        def _():
            for k in range(4):
                n = k if k < 3 else 4
                finish(n)
                if n > 1:
                    bring_home(n).start()

        @pl.when((s > 4) & (s <= UNITS))
        def _():
            n = unit_of(s - 1)
            finish(n)
            send_home(n)

        @pl.when(s == 2)
        def _():
            mixer_second()

        @pl.when(inside)
        def _():
            @pl.when(((s > 2) & (s < 6)) | (s == 8))
            def _():
                helper_dot(jnp.where(s == 8, 3, s - 3))

            @pl.when(((s > 3) & (s < 7)) | (s == 9))
            def _():
                helper_home(jnp.where(s == 9, 3, s - 4))

            @pl.when(((s > 5) & (s < 9)) | (s == 10))
            def _():
                helper_edge(jnp.where(s == 10, 3, s - 6))

        return carry

    small[4].wait()
    small[5].wait()
    lax.fori_loop(0, UNITS + 3, finish_step, 0)

    for h in range(2):
        rows = pl.ds(h * sub, sub)
        total = share(0, h) * acc[h, mine]
        for c in range(1, CHUNKS):
            n = 2 * c + h
            bring_home(n).wait_recv()
            total += share(c, h) * ret[n - 2]
        swap[h] = total

    @pl.when(end)
    def _():
        for k in range(GROUPS):
            edge_copy(k).wait_recv()
            for h in range(2):
                swap[h, :, pl.ds(k * wide, wide)] += edge_in[k, pl.ds(h * sub, sub)]

    for h in range(2):
        out[pl.ds(h * sub, sub)] = swap[h].astype(out.dtype)

    for j in range(LINES):

        @pl.when(z != j)
        def _():
            state_copy(j).wait_send()

    for copy in (*to_partner, *to_x, *to_y, *pass_x, *pass_y, *across.values()):
        copy.wait_send()
    for n in range(UNITS):
        own_in(n).wait_send()
        exchange(n).wait_send()
        if n > 1:
            bring_home(n).wait_send()

    @pl.when(inside)
    def _():
        for n in range(UNITS):
            own_out(n).wait_send()
            fwd_in(n).wait_send()
            fwd_out(n).wait_send()
        for k in range(GROUPS):
            exchange2(k).wait_send()
            edge_copy(k).wait_send()
            for c in range(1, CHUNKS):
                bring_home2(k, c).wait_send()

    @pl.when(end)
    def _():
        for k in range(GROUPS + 1):
            lend(k).wait_send()


def fused(
    seq_inputs,
    step_size,
    write_map,
    read_map,
    decay_log,
    skip_gain,
    moe_tokens,
    expert_ids,
    route_weights,
    gate_proj,
    up_proj,
    down_proj,
):
    rows, width = moe_tokens.shape
    part = gate_proj.shape[2]
    columns = down_proj.shape[2]
    length, lanes = seq_inputs.shape
    state_count = write_map.shape[0]
    block_count = length // BLOCK
    sub = rows // 2
    wide = columns // GROUPS
    dma = pltpu.SemaphoreType.DMA
    vmem = pl.BlockSpec(memory_space=pltpu.VMEM)
    smem = pl.BlockSpec(memory_space=pltpu.SMEM)
    hbm = pl.BlockSpec(memory_space=pl.ANY)
    return pl.pallas_call(
        fused_kernel,
        out_shape=(
            jax.ShapeDtypeStruct(seq_inputs.shape, BF16),
            jax.ShapeDtypeStruct((rows, columns), BF16),
        ),
        in_specs=[hbm] * 7 + [smem] * 2 + [hbm] * 3,
        out_specs=(vmem, vmem),
        scratch_shapes=[
            pltpu.VMEM((width, part), BF16),
            pltpu.VMEM((width, part), BF16),
            pltpu.VMEM((LINES, part, columns), BF16),
            pltpu.VMEM((UNITS, rows, width), BF16),
            pltpu.VMEM((LINES, UNITS, rows, part), BF16),
            pltpu.VMEM((UNITS, rows, columns), F32),
            pltpu.VMEM((UNITS, sub, columns), F32),
            pltpu.VMEM((UNITS - 2, sub, columns), F32),
            pltpu.VMEM((part, columns), BF16),
            pltpu.VMEM((GROUPS, UNITS, rows, wide), F32),
            pltpu.VMEM((GROUPS, UNITS, sub, wide), F32),
            pltpu.VMEM((GROUPS, CHUNKS - 1, 2, sub, wide), F32),
            pltpu.VMEM((GROUPS, rows, wide), F32),
            pltpu.VMEM((GROUPS, rows, wide), F32),
            pltpu.VMEM(expert_ids.shape, jnp.int32),
            pltpu.VMEM(route_weights.shape, F32),
            pltpu.VMEM(seq_inputs.shape, BF16),
            pltpu.VMEM(step_size.shape, F32),
            pltpu.VMEM(write_map.shape, BF16),
            pltpu.VMEM(read_map.shape, BF16),
            pltpu.VMEM((length, lanes), F32),
            pltpu.VMEM((length, lanes), F32),
            pltpu.VMEM((block_count, state_count, lanes), F32),
            pltpu.VMEM((block_count, 8, lanes), F32),
            pltpu.VMEM((state_count + 8, lanes), F32),
            pltpu.VMEM((LINES, state_count + 8, lanes), F32),
            dma((7,)),
            dma((6,)),
            dma((16,)),
            dma((16,)),
            dma((UNITS,)),
            dma((UNITS,)),
            dma((UNITS,)),
            dma((UNITS,)),
            dma((3, UNITS)),
            dma((GROUPS + 1,)),
            dma((GROUPS + 1,)),
            dma((GROUPS,)),
            dma((GROUPS,)),
            dma((UNITS,)),
            dma((UNITS,)),
            dma((UNITS,)),
            dma((UNITS,)),
            dma((GROUPS,)),
            dma((GROUPS,)),
            dma((GROUPS, CHUNKS)),
            dma((GROUPS, CHUNKS)),
            dma((LINES,)),
            dma((LINES,)),
        ],
        compiler_params=pltpu.CompilerParams(
            collective_id=0, has_side_effects=True, vmem_limit_bytes=VMEM_BYTES
        ),
    )(
        moe_tokens,
        expert_ids,
        route_weights,
        seq_inputs,
        step_size,
        write_map,
        read_map,
        decay_log,
        skip_gain,
        gate_proj[0],
        up_proj[0],
        down_proj[0].reshape(LINES, part, columns),
    )


def fits(moe_tokens, gate_proj, down_proj):
    return (
        lax.axis_size("exp") == PAIR * GRID * GRID
        and lax.axis_size("ctx") == LINES
        and gate_proj.shape[2] % 128 == 0
        and down_proj.shape[2] % 1024 == 0
        and moe_tokens.shape[0] % 128 == 0
    )


def on_device(
    seq_inputs,
    step_size,
    write_map,
    read_map,
    decay_log,
    skip_gain,
    moe_tokens,
    expert_ids,
    route_weights,
    gate_proj,
    up_proj,
    down_proj,
):
    if fits(moe_tokens, gate_proj, down_proj):
        return fused(
            seq_inputs,
            step_size,
            write_map,
            read_map,
            decay_log,
            skip_gain,
            moe_tokens,
            expert_ids,
            route_weights,
            gate_proj,
            up_proj,
            down_proj,
        )
    local_mix, cumulative, block_ends, entering, final = mixer_prepare(
        seq_inputs, step_size, write_map, read_map, decay_log
    )
    total_log = jnp.sum(block_ends, axis=1)
    head_count, state_count, head_width = final.shape
    logs = jnp.broadcast_to(total_log[:, None, None], (head_count, 8, head_width))
    packed = jnp.concatenate([final, logs], axis=1)
    gathered = lax.all_gather(packed, "ctx")
    expert_output = expert_block(
        moe_tokens, expert_ids, route_weights, gate_proj, up_proj, down_proj
    )
    place = lax.axis_index("ctx")
    state_before = jnp.zeros_like(final)
    for lap in range(lax.axis_size("ctx")):
        latter = gathered[lap]
        decay = jnp.exp(latter[:, state_count, 0])
        added = decay[:, None, None] * state_before + latter[:, :state_count]
        state_before = jnp.where(lap < place, added, state_before)
    mixer_output = mixer_finish(
        local_mix, cumulative, block_ends, entering, state_before, read_map, seq_inputs, skip_gain
    )
    return (mixer_output, expert_output)


def solution(mesh):
    return jax.shard_map(
        on_device,
        mesh=mesh,
        in_specs=(
            P("ctx", "exp"),
            P("exp", "ctx"),
            P(None, "ctx"),
            P(None, "ctx"),
            P("exp"),
            P("exp"),
            P("exp", None),
            P("exp", None),
            P("exp", None),
            P("exp", None, "ctx"),
            P("exp", None, "ctx"),
            P("exp", None, "ctx"),
        ),
        out_specs=(P("ctx", "exp"), P("exp", "ctx")),
        check_vma=False,
    )
```

time: 155 us -> 141 us (0.910)
  Pallas kernels: 141 us -> 134 us
  other arithmetic: 4.38 us -> 0 us
  matrix products: 2 us -> 0 us
    pallas_call x1, Pallas kernels: 141 us -> 134 us  [fused(): pl.pallas_call(fused_kernel, out_shape=(jax.ShapeDtypeStruct(seq_inputs.s...]
    unnamed x13 -> x4, local copies, waits for them, and re-layouts: 2.06 us -> 6.17 us
    reshape x4 -> x0, local copies, waits for them, and re-layouts: 2.95 us -> none  [the longest x2 1.49 us: mixer_prepare(): seq_inputs.reshape(block_count, BLOCK, head_count, head_width)]
    dot_general x5 -> x0, matrix products: 2 us -> none  [the longest x1 0.83 us: mixer_prepare(): jnp.einsum('hkts,kshp->kthp', mixing, value_blocks, preferred_element_typ...]
    mul x2 -> x0, other arithmetic: 1.55 us -> none  [the longest x1 0.79 us: mixer_prepare(): weights = jnp.exp(block_ends[:, :, None] - cumulative) * step_blocks]
where the time goes in v1:
time: 141 us
  Pallas kernels  134 us (95%)
  local copies, waits for them, and re-layouts  6.17 us (4%)
    pallas_call x1, Pallas kernels, fused(): pl.pallas_call(fused_kernel, out_shape=(jax.ShapeDtypeStruct(seq_inputs.s...  134 us
    unnamed x4, local copies, waits for them, and re-layouts  6.17 us

profile of v1, /device:TPU:0, one launch (start us, length us, event | category | flops | bytes accessed | tf_op | source)
XLA Modules:
  0.0 140.8 jit_solution(6123171808797851010)
XLA Ops:
  0.6 1.4 %copy.14.ids_hbm = s32[128,2]{1,0:T(8,128)} copy(s32[128,2]{0,1:T(2,128)} %param.19) | data formatting | bytes 2048 | tf_op args[7]
  2.0 1.4 %copy.15.route_hbm = f32[128,2]{1,0:T(8,128)} copy(f32[128,2]{0,1:T(2,128)} %param.20) | data formatting | bytes 2048 | tf_op args[8]
  3.5 134.0 %shard_map.131 = (bf16[512,256]{1,0:T(8,128)(2,1)}, bf16[128,1024]{1,0:T(8,128)(2,1)}) custom-call(bf16[128,4096]{1,0:T(8,128)(2,1)} %tok_hbm.1, s32[128,2]{1,0:T(8,128)} %copy.14.ids_hbm, f32[128,2]{1,0:T(8,128)} %copy.15.route_hbm, bf16[512,256]{1,0:T(8,128)(2,1)} %seq_hbm.1, f32[4,512]{1,0:T(4,128)} %step_hbm.1, bf16[16,512]{1,0:T(8,128)(2,1)} %write_hbm.1, ...), custom_call_target="tpu_custom_call" | custom-call | tf_op jit(solution)/shard_map/pallas_call | solution.py:798
  137.5 1.7 %copy.18 = bf16[512,256]{1,0:T(8,128)(2,1)} copy(bf16[512,256]{1,0:T(8,128)(2,1)} %get-tuple-element.4) | data formatting | bytes 524288
  139.2 1.7 %copy.19 = bf16[128,1024]{1,0:T(8,128)(2,1)} copy(bf16[128,1024]{1,0:T(8,128)(2,1)} %get-tuple-element.5) | data formatting | bytes 524288

commit v2 on v1

--- a/solution.py
+++ b/solution.py
@@ -125,13 +125,14 @@
 
 
 MESH = pl.DeviceIdType.MESH
-VMEM_BYTES = 61 * 2**20
+VMEM_BYTES = 58 * 2**20
 GRID = 2
 PAIR = 2
 LINES = 4
 CHUNKS = GRID * GRID
 UNITS = 2 * CHUNKS
-GROUPS = 4
+GROUPS = 8
+HELPED = UNITS - 2
 F32 = jnp.float32
 BF16 = jnp.bfloat16
 
@@ -148,8 +149,8 @@
     step_hbm,
     write_hbm,
     read_hbm,
-    decay_ref,
-    skip_ref,
+    decay_hbm,
+    skip_hbm,
     gate_hbm,
     up_hbm,
     down_hbm,
@@ -171,6 +172,9 @@
     edge_in,
     ids,
     route,
+    share,
+    decay_ref,
+    skip_ref,
     seq,
     step,
     write,
@@ -189,6 +193,7 @@
     own_out_send,
     fwd_in_send,
     fwd_out_send,
+    fwd_end_send,
     hrecv,
     wsend,
     wrecv,
@@ -211,7 +216,8 @@
     other = 1 - half
     px = lax.rem(e // PAIR, GRID)
     py = e // (PAIR * GRID)
-    sub = tok.shape[1] // 2
+    rows = tok.shape[1]
+    sub = rows // 2
     quarter = sub // 2
     part = gate_w.shape[1]
     first = part // 256 * 128
@@ -268,6 +274,8 @@
                 (seq_hbm, seq),
                 (ids_hbm, ids),
                 (route_hbm, route),
+                (decay_hbm, decay_ref),
+                (skip_hbm, skip_ref),
             ]
         )
     ]
@@ -325,10 +333,7 @@
         to_y[h].start()
 
     def lend(k):
-        if k < 2:
-            span = pl.ds(k * (wide // 2), wide // 2)
-        else:
-            span = pl.ds((k - 1) * wide, wide)
+        span = pl.ds(k * wide, wide)
         return remote(
             down_hbm.at[opposite, :, span], far_w.at[:, span], wsend.at[k], wrecv.at[k], (inner, e)
         )
@@ -354,6 +359,15 @@
     def fwd_out(n):
         return remote(
             hid.at[far, n], hid.at[far, n], fwd_out_send.at[n], hrecv.at[1, n], (outer, e)
+        )
+
+    def fwd_end(n):
+        return remote(
+            hid.at[opposite, n],
+            hid.at[opposite, n],
+            fwd_end_send.at[n - HELPED],
+            hrecv.at[2, n],
+            (outer, e),
         )
 
     def arrived(kind, j, n):
@@ -370,12 +384,12 @@
     lane_head = lax.broadcasted_iota(jnp.int32, (1, lanes), 1) // (lanes // head_count)
 
     def mixer_first():
-        for load in small[:4]:
+        for load in small:
             load.wait()
-        rows = lax.broadcasted_iota(jnp.int32, (BLOCK, BLOCK), 0)
-        cols = lax.broadcasted_iota(jnp.int32, (BLOCK, BLOCK), 1)
-        lower = cols <= rows
-        until = (rows <= cols).astype(F32)
+        down = lax.broadcasted_iota(jnp.int32, (BLOCK, BLOCK), 0)
+        over = lax.broadcasted_iota(jnp.int32, (BLOCK, BLOCK), 1)
+        lower = over <= down
+        until = (down <= over).astype(F32)
         since = lower.astype(F32)
         head_row = lax.broadcasted_iota(jnp.int32, (head_count, 1), 0)
         rate = jnp.zeros((head_count, 1), F32)
@@ -465,11 +479,19 @@
             total = local[span, :] + carried * grown[span, :] + gain * seq[span, :].astype(F32)
             mix_out[span, :] = total.astype(mix_out.dtype)
 
-    def share(c, h):
-        qx = lax.rem(px + c % GRID, GRID)
-        qy = lax.rem(py + c // GRID, GRID)
-        named = ids[h * sub : (h + 1) * sub, :] == qy * GRID + qx
-        return jnp.sum(jnp.where(named, route[h * sub : (h + 1) * sub, :], 0.0), axis=1, keepdims=True)
+    def make_share():
+        token = lax.broadcasted_iota(jnp.int32, (sub, rows), 1)
+        place = lax.broadcasted_iota(jnp.int32, (sub, rows), 0)
+        for c in range(CHUNKS):
+            qx = lax.rem(px + c % GRID, GRID)
+            qy = lax.rem(py + c // GRID, GRID)
+            chosen = jnp.where(ids[...] == qy * GRID + qx, route[...], 0.0)
+            weight = jnp.sum(chosen, axis=0, keepdims=True)
+            for h in range(2):
+                column = jnp.sum(
+                    jnp.where(token == place + h * sub, weight, 0.0), axis=1, keepdims=True
+                )
+                share[2 * c + h] = jnp.broadcast_to(column, (sub, 128))
 
     def add_down(j, n):
         acc[n] += jnp.dot(hid[j, n], down_w[j], preferred_element_type=F32)
@@ -496,10 +518,13 @@
         if t == 3 or t == 5:
             across[4 + (t - 3) // 2].wait_recv()
         if t >= 6:
+            across[t].wait_recv()
+
+    def tokens_ahead(t):
+        if t == 6 or t == 7:
             pass_x[t - 6].wait_recv()
             pass_y[t - 6].wait_recv()
             across[t].start()
-            across[t].wait_recv()
 
     def take_far(n):
         arrived(1, far, n)
@@ -510,7 +535,51 @@
 
         add_down(far, n)
 
+    def add_opposite(n):
+        arrived(2, opposite, n)
+
+        @pl.when(inside)
+        def _():
+            for k in range(HELPED, UNITS):
+
+                @pl.when(n == k)
+                def _():
+                    fwd_end(k).start()
+
+        add_down(opposite, n)
+
+    def take_near(n):
+        arrived(0, near, n)
+
+        @pl.when(inside)
+        def _():
+            fwd_in(n).start()
+
+        add_down(near, n)
+
+    def own_down(t, carry):
+        n = unit_of(t)
+        acc[n] = jnp.dot(hid[z, n], down_w[z], preferred_element_type=F32)
+        return carry
+
     def forward_step(t, carry):
+        @pl.when(t == 2)
+        def _():
+            loads[6].wait()
+
+        @pl.when((t > 1) & (t <= UNITS))
+        def _():
+            lax.fori_loop(jnp.where(t == 2, 0, t - 1), t, own_down, 0)
+
+        @pl.when(t == 2)
+        def _():
+            mixer_first()
+
+        @pl.when(inside & (t == 2))
+        def _():
+            take_near(0)
+            take_far(0)
+
         @pl.when(t < UNITS)
         def _():
             n = unit_of(t)
@@ -518,8 +587,6 @@
 
                 @pl.when(t == k)
                 def _():
-                    if k == 2:
-                        mixer_first()
                     tokens_ready(k)
 
             @pl.when(t == 0)
@@ -541,42 +608,40 @@
             def _():
                 own_out(n).start()
 
-            @pl.when(end | (t < 2))
+            @pl.when(end | (t == 0) | (t == 2) | (t == 3))
             def _():
                 own_in(n).start()
 
-            @pl.when(t == 0)
-            def _():
-                loads[6].wait()
-
-            acc[n] = jnp.dot(hid[z, n], down_w[z], preferred_element_type=F32)
-
-        @pl.when(t >= 2)
-        def _():
-            n = unit_of(t - 2)
-            arrived(0, near, n)
-
-            @pl.when(inside)
-            def _():
-                fwd_in(n).start()
-
-            add_down(near, n)
-
-        @pl.when(inside & (t > 3) & (t < 6))
-        def _():
-            take_far(t - 4)
-
-        @pl.when(t == UNITS - 1)
-        def _():
-            @pl.when(inside)
-            def _():
-                own_in(2).start()
-                own_in(4).start()
-
-            @pl.when(end)
-            def _():
-                for k in range(1, GROUPS + 1):
-                    lend(k).start()
+            for k in range(UNITS):
+
+                @pl.when(t == k)
+                def _():
+                    tokens_ahead(k + 1)
+
+        @pl.when(end & (t == 1))
+        def _():
+            lend(1).start()
+
+        @pl.when(end & (t == UNITS - 1))
+        def _():
+            for k in range(2, GROUPS):
+                lend(k).start()
+
+        @pl.when(inside & (t == UNITS))
+        def _():
+            def one(i, inner_carry):
+                add_opposite(unit_of(i))
+                return inner_carry
+
+            lax.fori_loop(0, 4, one, 0)
+
+        @pl.when(inside & (t > 2))
+        def _():
+            take_near(unit_of(t - 2))
+
+        @pl.when(inside & ((t == 4) | (t == 6)))
+        def _():
+            take_far(t - 2)
 
         return carry
 
@@ -584,7 +649,7 @@
 
     @pl.when(inside)
     def _():
-        for n in (3, 5, 6, 7):
+        for n in (6, 7, 3, 5, 1):
             own_in(n).start()
 
     def exchange(n):
@@ -596,13 +661,6 @@
     def finish(n):
         exchange(n).wait_recv()
         acc[n, mine] += swap[n]
-
-    def send_home(n):
-        for k in range(2, UNITS):
-
-            @pl.when(n == k)
-            def _():
-                bring_home(k).start()
 
     def exchange2(k):
         return remote(acc2.at[k, :, theirs], swap2.at[k], x2send.at[k], x2recv.at[k], partner)
@@ -620,111 +678,122 @@
         return remote(rsum.at[k], edge_in.at[k], rsend.at[k], rrecv.at[k], (outer, e))
 
     def helper_dot(k):
-        @pl.when(k == 0)
-        def _():
-            lend(0).wait_recv()
-            lend(1).wait_recv()
-
-        for i in range(1, GROUPS):
+        for i in range(GROUPS):
 
             @pl.when(k == i)
             def _():
-                lend(i + 1).wait_recv()
+                lend(i).wait_recv()
 
         span = pl.ds(pl.multiple_of(k * wide, wide), wide)
-
-        def one(n, carry):
-            acc2[k, n] = jnp.dot(hid[opposite, n], far_w[:, span], preferred_element_type=F32)
-            return carry
-
-        lax.fori_loop(0, UNITS, one, 0)
+        x = hid[opposite, pl.ds(0, HELPED)].reshape(HELPED * rows, part)
+        product = jnp.dot(x, far_w[:, span], preferred_element_type=F32)
+        acc2[k] = product.reshape(HELPED, rows, wide)
         exchange2(k).start()
 
     def helper_home(k):
         exchange2(k).wait_recv()
         acc2[k, :, mine] += swap2[k]
-        for c in range(1, CHUNKS):
+        for c in range(1, CHUNKS - 1):
             bring_home2(k, c).start()
 
     def helper_edge(k):
-        for c in range(1, CHUNKS):
+        for c in range(1, CHUNKS - 1):
             bring_home2(k, c).wait_recv()
         for h in range(2):
-            total = share(0, h) * acc2[k, h, mine]
-            for c in range(1, CHUNKS):
-                total += share(c, h) * ret2[k, c - 1, h]
+            total = share[h, :, 0:1] * acc2[k, h, mine]
+            for c in range(1, CHUNKS - 1):
+                total += share[2 * c + h, :, 0:1] * ret2[k, c - 1, h]
             rsum[k, pl.ds(h * sub, sub)] = total
         edge_copy(k).start()
 
+    make_share()
+
+    @pl.when(inside)
+    def _():
+        def one(i, carry):
+            add_opposite(unit_of(i))
+            return carry
+
+        lax.fori_loop(4, HELPED, one, 0)
+
+    @pl.when(end)
+    def _():
+        def near_one(n, carry):
+            take_near(n)
+            return carry
+
+        lax.fori_loop(0, UNITS, near_one, 0)
+
+        def far_one(i, carry):
+            take_far(2 * i)
+            return carry
+
+        lax.fori_loop(0, 3, far_one, 0)
+
+    for n in (0, 2, 4):
+        exchange(n).start()
+
+    @pl.when(inside)
+    def _():
+        helper_dot(0)
+        helper_dot(1)
+        helper_home(0)
+
+    for n in (0, 2, 4):
+        finish(n)
+        if n > 1:
+            bring_home(n).start()
+
+    order = (6, 7, 3, 5, 1)
+
     def finish_step(s, carry):
-        @pl.when((end & (s < UNITS)) | ((s > 1) & (s < UNITS)))
-        def _():
-            take_far(unit_of(s))
-
-        @pl.when(inside & (s > 1) & (s < 4))
-        def _():
-            def one(i, inner_carry):
-                n = unit_of((s - 2) * 4 + i)
-                arrived(2, opposite, n)
-                add_down(opposite, n)
-                return inner_carry
-
-            lax.fori_loop(0, 4, one, 0)
-
-        @pl.when(s == 3)
-        def _():
-            for k in range(4):
-                exchange(k if k < 3 else 4).start()
-
-        @pl.when((s > 3) & (s < UNITS))
-        def _():
-            exchange(unit_of(s)).start()
-
-        @pl.when(s == 4)
-        def _():
-            for k in range(4):
-                n = k if k < 3 else 4
-                finish(n)
-                if n > 1:
-                    bring_home(n).start()
-
-        @pl.when((s > 4) & (s <= UNITS))
-        def _():
-            n = unit_of(s - 1)
-            finish(n)
-            send_home(n)
-
-        @pl.when(s == 2)
+        @pl.when(s < 2)
+        def _():
+            add_opposite(HELPED + s)
+
+        n = jnp.where(s < 4, HELPED + s - 2, jnp.where(s < 6, 2 * s - 5, 1))
+
+        @pl.when((s > 1) & (s < 7))
+        def _():
+            take_far(n)
+            exchange(n).start()
+
+        @pl.when(inside)
+        def _():
+            @pl.when(s < GROUPS - 2)
+            def _():
+                helper_dot(s + 2)
+
+            @pl.when(s < GROUPS - 1)
+            def _():
+                helper_home(s + 1)
+
+        for i, unit in enumerate(order):
+
+            @pl.when(s == i + 2)
+            def _():
+                finish(unit)
+                if unit > 1:
+                    bring_home(unit).start()
+
+        @pl.when(s == 0)
         def _():
             mixer_second()
 
         @pl.when(inside)
         def _():
-            @pl.when(((s > 2) & (s < 6)) | (s == 8))
-            def _():
-                helper_dot(jnp.where(s == 8, 3, s - 3))
-
-            @pl.when(((s > 3) & (s < 7)) | (s == 9))
-            def _():
-                helper_home(jnp.where(s == 9, 3, s - 4))
-
-            @pl.when(((s > 5) & (s < 9)) | (s == 10))
-            def _():
-                helper_edge(jnp.where(s == 10, 3, s - 6))
+            helper_edge(s)
 
         return carry
 
-    small[4].wait()
-    small[5].wait()
-    lax.fori_loop(0, UNITS + 3, finish_step, 0)
+    lax.fori_loop(0, GROUPS, finish_step, 0)
 
     for h in range(2):
-        rows = pl.ds(h * sub, sub)
-        total = share(0, h) * acc[h, mine]
+        total = share[h, :, 0:1] * acc[h, mine]
         for c in range(1, CHUNKS):
             n = 2 * c + h
             bring_home(n).wait_recv()
-            total += share(c, h) * ret[n - 2]
+            total += share[n, :, 0:1] * ret[n - 2]
         swap[h] = total
 
     @pl.when(end)
@@ -760,12 +829,14 @@
         for k in range(GROUPS):
             exchange2(k).wait_send()
             edge_copy(k).wait_send()
-            for c in range(1, CHUNKS):
+            for c in range(1, CHUNKS - 1):
                 bring_home2(k, c).wait_send()
+        for n in range(HELPED, UNITS):
+            fwd_end(n).wait_send()
 
     @pl.when(end)
     def _():
-        for k in range(GROUPS + 1):
+        for k in range(GROUPS):
             lend(k).wait_send()
 
 
@@ -793,7 +864,6 @@
     wide = columns // GROUPS
     dma = pltpu.SemaphoreType.DMA
     vmem = pl.BlockSpec(memory_space=pltpu.VMEM)
-    smem = pl.BlockSpec(memory_space=pltpu.SMEM)
     hbm = pl.BlockSpec(memory_space=pl.ANY)
     return pl.pallas_call(
         fused_kernel,
@@ -801,7 +871,7 @@
             jax.ShapeDtypeStruct(seq_inputs.shape, BF16),
             jax.ShapeDtypeStruct((rows, columns), BF16),
         ),
-        in_specs=[hbm] * 7 + [smem] * 2 + [hbm] * 3,
+        in_specs=[hbm] * 12,
         out_specs=(vmem, vmem),
         scratch_shapes=[
             pltpu.VMEM((width, part), BF16),
@@ -813,13 +883,16 @@
             pltpu.VMEM((UNITS, sub, columns), F32),
             pltpu.VMEM((UNITS - 2, sub, columns), F32),
             pltpu.VMEM((part, columns), BF16),
-            pltpu.VMEM((GROUPS, UNITS, rows, wide), F32),
-            pltpu.VMEM((GROUPS, UNITS, sub, wide), F32),
-            pltpu.VMEM((GROUPS, CHUNKS - 1, 2, sub, wide), F32),
+            pltpu.VMEM((GROUPS, HELPED, rows, wide), F32),
+            pltpu.VMEM((GROUPS, HELPED, sub, wide), F32),
+            pltpu.VMEM((GROUPS, CHUNKS - 2, 2, sub, wide), F32),
             pltpu.VMEM((GROUPS, rows, wide), F32),
             pltpu.VMEM((GROUPS, rows, wide), F32),
-            pltpu.VMEM(expert_ids.shape, jnp.int32),
-            pltpu.VMEM(route_weights.shape, F32),
+            pltpu.VMEM((2, rows), jnp.int32),
+            pltpu.VMEM((2, rows), F32),
+            pltpu.VMEM((UNITS, sub, 128), F32),
+            pltpu.SMEM(decay_log.shape, F32),
+            pltpu.SMEM(skip_gain.shape, F32),
             pltpu.VMEM(seq_inputs.shape, BF16),
             pltpu.VMEM(step_size.shape, F32),
             pltpu.VMEM(write_map.shape, BF16),
@@ -831,16 +904,17 @@
             pltpu.VMEM((state_count + 8, lanes), F32),
             pltpu.VMEM((LINES, state_count + 8, lanes), F32),
             dma((7,)),
-            dma((6,)),
+            dma((8,)),
             dma((16,)),
             dma((16,)),
             dma((UNITS,)),
             dma((UNITS,)),
             dma((UNITS,)),
             dma((UNITS,)),
+            dma((2,)),
             dma((3, UNITS)),
-            dma((GROUPS + 1,)),
-            dma((GROUPS + 1,)),
+            dma((GROUPS,)),
+            dma((GROUPS,)),
             dma((GROUPS,)),
             dma((GROUPS,)),
             dma((UNITS,)),
@@ -859,8 +933,8 @@
         ),
     )(
         moe_tokens,
-        expert_ids,
-        route_weights,
+        expert_ids.T,
+        route_weights.T,
         seq_inputs,
         step_size,
         write_map,
@@ -879,7 +953,7 @@
         and lax.axis_size("ctx") == LINES
         and gate_proj.shape[2] % 128 == 0
         and down_proj.shape[2] % 1024 == 0
-        and moe_tokens.shape[0] % 128 == 0
+        and moe_tokens.shape[0] == 128
     )
 
 

time: 141 us -> 121 us (0.86)
  Pallas kernels: 134 us -> 116 us
  local copies, waits for them, and re-layouts: 6.17 us -> 3.34 us
    pallas_call x1, Pallas kernels: 134 us -> 116 us  [fused(): pl.pallas_call(fused_kernel, out_shape=(jax.ShapeDtypeStruct(seq_inputs.s...]
    unnamed x4 -> x2, local copies, waits for them, and re-layouts: 6.17 us -> 3.34 us
where the time goes in v2:
time: 121 us; the launch traced here: 120 us
  Pallas kernels  116 us (96%)
  local copies, waits for them, and re-layouts  3.34 us (3%)
    pallas_call x1, Pallas kernels, fused(): pl.pallas_call(fused_kernel, out_shape=(jax.ShapeDtypeStruct(seq_inputs.s...  116 us
    unnamed x2, local copies, waits for them, and re-layouts  3.34 us

profile of v2, /device:TPU:0, one launch (start us, length us, event | category | flops | bytes accessed | tf_op | source)
XLA Modules:
  0.0 120.4 jit_solution(1495490293204599647)
XLA Ops:
  0.6 116.4 %shard_map.131 = (bf16[512,256]{1,0:T(8,128)(2,1)}, bf16[128,1024]{1,0:T(8,128)(2,1)}) custom-call(bf16[128,4096]{1,0:T(8,128)(2,1)} %tok_hbm.1, s32[2,128]{1,0:T(2,128)} %bitcast.8, f32[2,128]{1,0:T(2,128)} %bitcast.9, bf16[512,256]{1,0:T(8,128)(2,1)} %seq_hbm.1, f32[4,512]{1,0:T(4,128)} %step_hbm.1, bf16[16,512]{1,0:T(8,128)(2,1)} %write_hbm.1, ...), custom_call_target="tpu_custom_call" | custom-call | tf_op jit(solution)/shard_map/pallas_call | solution.py:868
  117.0 1.7 %copy.16 = bf16[512,256]{1,0:T(8,128)(2,1)} copy(bf16[512,256]{1,0:T(8,128)(2,1)} %get-tuple-element.4) | data formatting | bytes 524288
  118.7 1.7 %copy.17 = bf16[128,1024]{1,0:T(8,128)(2,1)} copy(bf16[128,1024]{1,0:T(8,128)(2,1)} %get-tuple-element.5) | data formatting | bytes 524288

commit v3 on v2

--- a/solution.py
+++ b/solution.py
@@ -154,6 +154,8 @@
     gate_hbm,
     up_hbm,
     down_hbm,
+    mix_hbm,
+    out_hbm,
     mix_out,
     out,
     gate_w,
@@ -168,8 +170,7 @@
     acc2,
     swap2,
     ret2,
-    rsum,
-    edge_in,
+    edge,
     ids,
     route,
     share,
@@ -183,8 +184,9 @@
     grown,
     entering,
     before,
-    packed,
-    states,
+    final,
+    came,
+    passed,
     load_sem,
     small_sem,
     tsend,
@@ -287,13 +289,16 @@
     barrier = pltpu.get_barrier_semaphore()
     for device in (partner, peer(1, half), peer(2, half), peer(3, half)):
         pl.semaphore_signal(barrier, inc=1, device_id=device, device_id_type=MESH)
-    for j in range(LINES):
-
-        @pl.when(z != j)
-        def _():
-            pl.semaphore_signal(barrier, inc=1, device_id=(j, e), device_id_type=MESH)
-
-    pl.semaphore_wait(barrier, 4 + LINES - 1)
+    pl.semaphore_signal(barrier, inc=1, device_id=(inner, e), device_id_type=MESH)
+
+    @pl.when(inside)
+    def _():
+        pl.semaphore_signal(barrier, inc=1, device_id=(outer, e), device_id_type=MESH)
+        pl.semaphore_wait(barrier, 6)
+
+    @pl.when(end)
+    def _():
+        pl.semaphore_wait(barrier, 5)
 
     def tok_rows(h):
         return tok_hbm.at[pl.ds(h * sub, sub)]
@@ -332,24 +337,41 @@
         to_x[h].start()
         to_y[h].start()
 
-    def lend(k):
+    def lend(k, begin=0, count=part):
         span = pl.ds(k * wide, wide)
+        line = pl.ds(begin, count)
         return remote(
-            down_hbm.at[opposite, :, span], far_w.at[:, span], wsend.at[k], wrecv.at[k], (inner, e)
+            down_hbm.at[opposite, line, span],
+            far_w.at[line, span],
+            wsend.at[k],
+            wrecv.at[k],
+            (inner, e),
         )
 
     @pl.when(end)
     def _():
-        lend(0).start()
-
-    def own_in(n):
+        lend(0, 0, part // 2).start()
+
+    whole = pl.ds(0, part)
+
+    def own_in(n, span=whole):
         kind = jnp.where(end, 0, 1)
         return remote(
-            hid.at[z, n], hid.at[z, n], own_in_send.at[n], hrecv.at[kind, n], (inner, e)
+            hid.at[z, n, :, span],
+            hid.at[z, n, :, span],
+            own_in_send.at[n],
+            hrecv.at[kind, n],
+            (inner, e),
         )
 
-    def own_out(n):
-        return remote(hid.at[z, n], hid.at[z, n], own_out_send.at[n], hrecv.at[0, n], (outer, e))
+    def own_out(n, span=whole):
+        return remote(
+            hid.at[z, n, :, span],
+            hid.at[z, n, :, span],
+            own_out_send.at[n],
+            hrecv.at[0, n],
+            (outer, e),
+        )
 
     def fwd_in(n):
         return remote(
@@ -373,8 +395,11 @@
     def arrived(kind, j, n):
         remote(hid.at[j, n], hid.at[j, n], own_in_send.at[n], hrecv.at[kind, n], (near, e)).wait_recv()
 
-    def state_copy(j):
-        return remote(packed, states.at[z], ssend.at[j], srecv.at[z], (j, e))
+    def state_copy():
+        return remote(passed, came, ssend.at[0], srecv.at[0], (z + 1, e))
+
+    def state_back():
+        return remote(passed, came, ssend.at[0], srecv.at[0], (z - 1, e))
 
     head_count = step.shape[0]
     length = step.shape[1]
@@ -382,6 +407,9 @@
     lanes = seq.shape[1]
     block_count = length // BLOCK
     lane_head = lax.broadcasted_iota(jnp.int32, (1, lanes), 1) // (lanes // head_count)
+
+    mix_copy = pltpu.make_async_copy(mix_out, mix_hbm, load_sem.at[7])
+    out_copy = pltpu.make_async_copy(out, out_hbm, load_sem.at[8])
 
     def mixer_first():
         for load in small:
@@ -442,27 +470,26 @@
             before[k] = jnp.broadcast_to(gone, (8, lanes))
             state = jnp.exp(ends) * state + increment
             gone = gone + ends
-        packed[0:state_count, :] = state
-        packed[state_count:, :] = jnp.broadcast_to(gone, (8, lanes))
-        states[z] = packed[...]
-        for j in range(LINES):
-
-            @pl.when(z != j)
-            def _():
-                state_copy(j).start()
+        final[...] = state
+        before[block_count] = jnp.broadcast_to(gone, (8, lanes))
+
+        @pl.when(z == 0)
+        def _():
+            came[...] = jnp.zeros((state_count, lanes), F32)
+            passed[...] = state
+            state_copy().start()
+
+    def mixer_pass():
+        state_back().wait_recv()
+        passed[...] = jnp.exp(before[block_count][0:1, :]) * came[...] + final[...]
+        state_copy().start()
 
     def mixer_second():
-        for j in range(LINES):
-
-            @pl.when(z != j)
-            def _():
-                remote(packed, states.at[j], ssend.at[j], srecv.at[j], (j, e)).wait_recv()
-
-        state = jnp.zeros((state_count, lanes), F32)
-        for lap in range(LINES):
-            latter = states[lap]
-            added = jnp.exp(latter[state_count : state_count + 1, :]) * state + latter[:state_count, :]
-            state = jnp.where(lap < z, added, state)
+        @pl.when(z == LINES - 1)
+        def _():
+            state_back().wait_recv()
+
+        state = came[...]
         gain = jnp.zeros((1, lanes), F32)
         for h in range(head_count):
             gain = jnp.where(lane_head == h, skip_ref[h], gain)
@@ -478,6 +505,7 @@
             )
             total = local[span, :] + carried * grown[span, :] + gain * seq[span, :].astype(F32)
             mix_out[span, :] = total.astype(mix_out.dtype)
+        mix_copy.start()
 
     def make_share():
         token = lax.broadcasted_iota(jnp.int32, (sub, rows), 1)
@@ -562,6 +590,22 @@
         acc[n] = jnp.dot(hid[z, n], down_w[z], preferred_element_type=F32)
         return carry
 
+    def exchange(n):
+        return remote(acc.at[n, theirs], swap.at[n], xsend.at[n], xrecv.at[n], partner)
+
+    def bring_home(n):
+        return remote(acc.at[n, mine], ret.at[n - 2], bsend.at[n], brecv.at[n], peer(n // 2, half))
+
+    def finish(n):
+        exchange(n).wait_recv()
+        acc[n, mine] += swap[n]
+
+    def early_finish():
+        for n in (0, 2, 4):
+            finish(n)
+            if n > 1:
+                bring_home(n).start()
+
     def forward_step(t, carry):
         @pl.when(t == 2)
         def _():
@@ -574,6 +618,10 @@
         @pl.when(t == 2)
         def _():
             mixer_first()
+
+        @pl.when(((z == 1) & (t == 4)) | ((z == 2) & (t == 6)))
+        def _():
+            mixer_pass()
 
         @pl.when(inside & (t == 2))
         def _():
@@ -588,6 +636,11 @@
                 @pl.when(t == k)
                 def _():
                     tokens_ready(k)
+                    if k == 2:
+
+                        @pl.when(inside)
+                        def _():
+                            take_near(1)
 
             @pl.when(t == 0)
             def _():
@@ -598,17 +651,31 @@
 
             @pl.when(t == 0)
             def _():
+                own_in(0, left).start()
+
+                @pl.when(inside)
+                def _():
+                    own_out(0, left).start()
+
                 loads[3].wait()
                 loads[4].wait()
                 loads[6].start()
 
             make_hidden(n, right)
 
-            @pl.when(inside)
+            @pl.when(t == 0)
+            def _():
+                own_in(0, right).start()
+
+                @pl.when(inside)
+                def _():
+                    own_out(0, right).start()
+
+            @pl.when(inside & (t > 0))
             def _():
                 own_out(n).start()
 
-            @pl.when(end | (t == 0) | (t == 2) | (t == 3))
+            @pl.when((end & (t > 0)) | (t == 2) | (t == 3))
             def _():
                 own_in(n).start()
 
@@ -620,11 +687,11 @@
 
         @pl.when(end & (t == 1))
         def _():
-            lend(1).start()
+            lend(0, part // 2, part - part // 2).start()
 
         @pl.when(end & (t == UNITS - 1))
         def _():
-            for k in range(2, GROUPS):
+            for k in range(1, GROUPS):
                 lend(k).start()
 
         @pl.when(inside & (t == UNITS))
@@ -634,8 +701,14 @@
                 return inner_carry
 
             lax.fori_loop(0, 4, one, 0)
-
-        @pl.when(inside & (t > 2))
+            for n in (0, 2, 4):
+                exchange(n).start()
+
+        @pl.when(inside & (t == UNITS + 1))
+        def _():
+            early_finish()
+
+        @pl.when(inside & (t > 3))
         def _():
             take_near(unit_of(t - 2))
 
@@ -651,16 +724,6 @@
     def _():
         for n in (6, 7, 3, 5, 1):
             own_in(n).start()
-
-    def exchange(n):
-        return remote(acc.at[n, theirs], swap.at[n], xsend.at[n], xrecv.at[n], partner)
-
-    def bring_home(n):
-        return remote(acc.at[n, mine], ret.at[n - 2], bsend.at[n], brecv.at[n], peer(n // 2, half))
-
-    def finish(n):
-        exchange(n).wait_recv()
-        acc[n, mine] += swap[n]
 
     def exchange2(k):
         return remote(acc2.at[k, :, theirs], swap2.at[k], x2send.at[k], x2recv.at[k], partner)
@@ -675,7 +738,7 @@
         )
 
     def edge_copy(k):
-        return remote(rsum.at[k], edge_in.at[k], rsend.at[k], rrecv.at[k], (outer, e))
+        return remote(edge.at[k], edge.at[k], rsend.at[k], rrecv.at[k], (outer, e))
 
     def helper_dot(k):
         for i in range(GROUPS):
@@ -703,7 +766,7 @@
             total = share[h, :, 0:1] * acc2[k, h, mine]
             for c in range(1, CHUNKS - 1):
                 total += share[2 * c + h, :, 0:1] * ret2[k, c - 1, h]
-            rsum[k, pl.ds(h * sub, sub)] = total
+            edge[k, pl.ds(h * sub, sub)] = total.astype(edge.dtype)
         edge_copy(k).start()
 
     make_share()
@@ -729,25 +792,22 @@
             return carry
 
         lax.fori_loop(0, 3, far_one, 0)
-
-    for n in (0, 2, 4):
-        exchange(n).start()
+        for n in (0, 2, 4):
+            exchange(n).start()
+        early_finish()
 
     @pl.when(inside)
     def _():
+        add_opposite(HELPED)
         helper_dot(0)
         helper_dot(1)
         helper_home(0)
 
-    for n in (0, 2, 4):
-        finish(n)
-        if n > 1:
-            bring_home(n).start()
-
     order = (6, 7, 3, 5, 1)
+    home = (2, 4, 6, 6)
 
     def finish_step(s, carry):
-        @pl.when(s < 2)
+        @pl.when((s == 1) | (end & (s == 0)))
         def _():
             add_opposite(HELPED + s)
 
@@ -760,11 +820,11 @@
 
         @pl.when(inside)
         def _():
-            @pl.when(s < GROUPS - 2)
+            @pl.when(s < 6)
             def _():
                 helper_dot(s + 2)
 
-            @pl.when(s < GROUPS - 1)
+            @pl.when(s < 7)
             def _():
                 helper_home(s + 1)
 
@@ -773,20 +833,24 @@
             @pl.when(s == i + 2)
             def _():
                 finish(unit)
-                if unit > 1:
+
+            if unit > 1:
+
+                @pl.when(s == jnp.where(inside, home[i], i + 2))
+                def _():
                     bring_home(unit).start()
 
         @pl.when(s == 0)
         def _():
             mixer_second()
 
-        @pl.when(inside)
-        def _():
-            helper_edge(s)
+        @pl.when(inside & (s > 6))
+        def _():
+            helper_edge(s - 7)
 
         return carry
 
-    lax.fori_loop(0, GROUPS, finish_step, 0)
+    lax.fori_loop(0, GROUPS + 7, finish_step, 0)
 
     for h in range(2):
         total = share[h, :, 0:1] * acc[h, mine]
@@ -800,17 +864,20 @@
     def _():
         for k in range(GROUPS):
             edge_copy(k).wait_recv()
+            span = pl.ds(k * wide, wide)
             for h in range(2):
-                swap[h, :, pl.ds(k * wide, wide)] += edge_in[k, pl.ds(h * sub, sub)]
-
-    for h in range(2):
-        out[pl.ds(h * sub, sub)] = swap[h].astype(out.dtype)
-
-    for j in range(LINES):
-
-        @pl.when(z != j)
-        def _():
-            state_copy(j).wait_send()
+                line = pl.ds(h * sub, sub)
+                out[line, span] = (swap[h, :, span] + edge[k, line].astype(F32)).astype(out.dtype)
+
+    @pl.when(inside)
+    def _():
+        for h in range(2):
+            out[pl.ds(h * sub, sub)] = swap[h].astype(out.dtype)
+
+    out_copy.start()
+    @pl.when(z < LINES - 1)
+    def _():
+        state_copy().wait_send()
 
     for copy in (*to_partner, *to_x, *to_y, *pass_x, *pass_y, *across.values()):
         copy.wait_send()
@@ -838,6 +905,9 @@
     def _():
         for k in range(GROUPS):
             lend(k).wait_send()
+
+    mix_copy.wait()
+    out_copy.wait()
 
 
 def fused(
@@ -863,17 +933,18 @@
     sub = rows // 2
     wide = columns // GROUPS
     dma = pltpu.SemaphoreType.DMA
-    vmem = pl.BlockSpec(memory_space=pltpu.VMEM)
     hbm = pl.BlockSpec(memory_space=pl.ANY)
-    return pl.pallas_call(
+    results = pl.pallas_call(
         fused_kernel,
         out_shape=(
             jax.ShapeDtypeStruct(seq_inputs.shape, BF16),
             jax.ShapeDtypeStruct((rows, columns), BF16),
         ),
         in_specs=[hbm] * 12,
-        out_specs=(vmem, vmem),
+        out_specs=(hbm, hbm),
         scratch_shapes=[
+            pltpu.VMEM(seq_inputs.shape, BF16),
+            pltpu.VMEM((rows, columns), BF16),
             pltpu.VMEM((width, part), BF16),
             pltpu.VMEM((width, part), BF16),
             pltpu.VMEM((LINES, part, columns), BF16),
@@ -886,8 +957,7 @@
             pltpu.VMEM((GROUPS, HELPED, rows, wide), F32),
             pltpu.VMEM((GROUPS, HELPED, sub, wide), F32),
             pltpu.VMEM((GROUPS, CHUNKS - 2, 2, sub, wide), F32),
-            pltpu.VMEM((GROUPS, rows, wide), F32),
-            pltpu.VMEM((GROUPS, rows, wide), F32),
+            pltpu.VMEM((GROUPS, rows, wide), BF16),
             pltpu.VMEM((2, rows), jnp.int32),
             pltpu.VMEM((2, rows), F32),
             pltpu.VMEM((UNITS, sub, 128), F32),
@@ -900,10 +970,11 @@
             pltpu.VMEM((length, lanes), F32),
             pltpu.VMEM((length, lanes), F32),
             pltpu.VMEM((block_count, state_count, lanes), F32),
-            pltpu.VMEM((block_count, 8, lanes), F32),
-            pltpu.VMEM((state_count + 8, lanes), F32),
-            pltpu.VMEM((LINES, state_count + 8, lanes), F32),
-            dma((7,)),
+            pltpu.VMEM((block_count + 1, 8, lanes), F32),
+            pltpu.VMEM((state_count, lanes), F32),
+            pltpu.VMEM((state_count, lanes), F32),
+            pltpu.VMEM((state_count, lanes), F32),
+            dma((9,)),
             dma((8,)),
             dma((16,)),
             dma((16,)),
@@ -925,8 +996,8 @@
             dma((GROUPS,)),
             dma((GROUPS, CHUNKS)),
             dma((GROUPS, CHUNKS)),
-            dma((LINES,)),
-            dma((LINES,)),
+            dma((1,)),
+            dma((1,)),
         ],
         compiler_params=pltpu.CompilerParams(
             collective_id=0, has_side_effects=True, vmem_limit_bytes=VMEM_BYTES
@@ -945,6 +1016,46 @@
         up_proj[0],
         down_proj[0].reshape(LINES, part, columns),
     )
+    return hand_over(*results)
+
+
+def hand_over_kernel(*refs):
+    count = (len(refs) - 2) // 3
+    sources, targets, held = refs[:count], refs[count : 2 * count], refs[2 * count : 3 * count]
+    in_sem, out_sem = refs[3 * count :]
+    pieces = in_sem.shape[1]
+    loads, stores = [], []
+    for i in range(count):
+        step = held[i].shape[0] // pieces
+        for k in range(pieces):
+            line = pl.ds(k * step, step)
+            loads.append(
+                pltpu.make_async_copy(sources[i].at[line], held[i].at[line], in_sem.at[i, k])
+            )
+            stores.append(
+                pltpu.make_async_copy(held[i].at[line], targets[i].at[line], out_sem.at[i, k])
+            )
+    for load in loads:
+        load.start()
+    for load, store in zip(loads, stores):
+        load.wait()
+        store.start()
+    for store in stores:
+        store.wait()
+
+
+def hand_over(*arrays):
+    hbm = pl.BlockSpec(memory_space=pltpu.HBM)
+    pieces = 2
+    dma = pltpu.SemaphoreType.DMA((len(arrays), pieces))
+    return pl.pallas_call(
+        hand_over_kernel,
+        out_shape=tuple(jax.ShapeDtypeStruct(a.shape, a.dtype) for a in arrays),
+        in_specs=[hbm] * len(arrays),
+        out_specs=(hbm,) * len(arrays),
+        scratch_shapes=[pltpu.VMEM(a.shape, a.dtype) for a in arrays] + [dma, dma],
+        compiler_params=pltpu.CompilerParams(vmem_limit_bytes=VMEM_BYTES),
+    )(*arrays)
 
 
 def fits(moe_tokens, gate_proj, down_proj):

time: 121 us -> 110 us (0.909)
  Pallas kernels: 116 us -> 109 us
  local copies, waits for them, and re-layouts: 3.34 us -> 0 us
    pallas_call x1, Pallas kernels: 116 us -> 107 us  [fused(): pl.pallas_call(fused_kernel, out_shape=(jax.ShapeDtypeStruct(seq_inputs.s...]
    unnamed x2 -> x0, local copies, waits for them, and re-layouts: 3.34 us -> none
    pallas_call x0 -> x1, Pallas kernels: none -> 1.82 us  [hand_over(): pl.pallas_call(hand_over_kernel, out_shape=tuple((jax.ShapeDtypeStruct(a....]
where the time goes in v3:
time: 110 us; the launch traced here: 109 us
  Pallas kernels  109 us (99%)
    pallas_call x1, Pallas kernels, fused(): pl.pallas_call(fused_kernel, out_shape=(jax.ShapeDtypeStruct(seq_inputs.s...  107 us

profile of v3, /device:TPU:0, one launch (start us, length us, event | category | flops | bytes accessed | tf_op | source)
XLA Modules:
  0.0 109.5 jit_solution(7767334280030569105)
XLA Ops:
  0.6 107.0 %shard_map.131 = (bf16[512,256]{1,0:T(8,128)(2,1)}, bf16[128,1024]{1,0:T(8,128)(2,1)}) custom-call(bf16[128,4096]{1,0:T(8,128)(2,1)} %tok_hbm.1, s32[2,128]{1,0:T(2,128)} %bitcast.8, f32[2,128]{1,0:T(2,128)} %bitcast.9, bf16[512,256]{1,0:T(8,128)(2,1)} %seq_hbm.1, f32[4,512]{1,0:T(4,128)} %step_hbm.1, bf16[16,512]{1,0:T(8,128)(2,1)} %write_hbm.1, ...), custom_call_target="tpu_custom_call" | custom-call | tf_op jit(solution)/shard_map/pallas_call | solution.py:937
  107.7 1.8 %shard_map.132 = (bf16[512,256]{1,0:T(8,128)(2,1)}, bf16[128,1024]{1,0:T(8,128)(2,1)}) custom-call(bf16[512,256]{1,0:T(8,128)(2,1)} %get-tuple-element.4.refs_0_, bf16[128,1024]{1,0:T(8,128)(2,1)} %get-tuple-element.5.refs_1_), custom_call_target="tpu_custom_call" | custom-call | tf_op jit(solution)/shard_map/pallas_call | solution.py:1051

commit v4 on v3

--- a/solution.py
+++ b/solution.py
@@ -304,32 +304,32 @@
         return tok_hbm.at[pl.ds(h * sub, sub)]
 
     to_partner = [
-        remote(tok_rows(h), tok.at[h, mine], tsend.at[h], trecv.at[h], partner) for h in range(2)
+        remote(tok_rows(h), tok.at[h, mine], tsend.at[0], trecv.at[h], partner) for h in range(2)
     ]
     to_x = [
-        remote(tok_rows(h), tok.at[2 + h, mine], tsend.at[2 + h], trecv.at[2 + h], peer(1, half))
+        remote(tok_rows(h), tok.at[2 + h, mine], tsend.at[0], trecv.at[2 + h], peer(1, half))
         for h in range(2)
     ]
     to_y = [
-        remote(tok_rows(h), tok.at[4 + h, mine], tsend.at[4 + h], trecv.at[4 + h], peer(2, half))
+        remote(tok_rows(h), tok.at[4 + h, mine], tsend.at[0], trecv.at[4 + h], peer(2, half))
         for h in range(2)
     ]
     pass_x = [
         remote(
-            tok.at[4 + h, mine_a], tok.at[6 + h, mine_a], tsend.at[6 + h], trecv.at[6 + h],
+            tok.at[4 + h, mine_a], tok.at[6 + h, mine_a], tsend.at[0], trecv.at[6 + h],
             peer(1, half),
         )
         for h in range(2)
     ]
     pass_y = [
         remote(
-            tok.at[2 + h, mine_b], tok.at[6 + h, mine_b], tsend.at[8 + h], trecv.at[8 + h],
+            tok.at[2 + h, mine_b], tok.at[6 + h, mine_b], tsend.at[0], trecv.at[8 + h],
             peer(2, half),
         )
         for h in range(2)
     ]
     across = {
-        n: remote(tok.at[n, mine], tok.at[n, mine], tsend.at[8 + n], trecv.at[8 + n], partner)
+        n: remote(tok.at[n, mine], tok.at[n, mine], tsend.at[0], trecv.at[8 + n], partner)
         for n in range(2, UNITS)
     }
     for h in range(2):
@@ -343,7 +343,7 @@
         return remote(
             down_hbm.at[opposite, line, span],
             far_w.at[line, span],
-            wsend.at[k],
+            wsend.at[0],
             wrecv.at[k],
             (inner, e),
         )
@@ -359,7 +359,7 @@
         return remote(
             hid.at[z, n, :, span],
             hid.at[z, n, :, span],
-            own_in_send.at[n],
+            own_in_send.at[0],
             hrecv.at[kind, n],
             (inner, e),
         )
@@ -368,32 +368,32 @@
         return remote(
             hid.at[z, n, :, span],
             hid.at[z, n, :, span],
-            own_out_send.at[n],
+            own_out_send.at[0],
             hrecv.at[0, n],
             (outer, e),
         )
 
     def fwd_in(n):
         return remote(
-            hid.at[near, n], hid.at[near, n], fwd_in_send.at[n], hrecv.at[2, n], (inner, e)
+            hid.at[near, n], hid.at[near, n], fwd_in_send.at[0], hrecv.at[2, n], (inner, e)
         )
 
     def fwd_out(n):
         return remote(
-            hid.at[far, n], hid.at[far, n], fwd_out_send.at[n], hrecv.at[1, n], (outer, e)
+            hid.at[far, n], hid.at[far, n], fwd_out_send.at[0], hrecv.at[1, n], (outer, e)
         )
 
     def fwd_end(n):
         return remote(
             hid.at[opposite, n],
             hid.at[opposite, n],
-            fwd_end_send.at[n - HELPED],
+            fwd_end_send.at[0],
             hrecv.at[2, n],
             (outer, e),
         )
 
     def arrived(kind, j, n):
-        remote(hid.at[j, n], hid.at[j, n], own_in_send.at[n], hrecv.at[kind, n], (near, e)).wait_recv()
+        remote(hid.at[j, n], hid.at[j, n], own_in_send.at[0], hrecv.at[kind, n], (near, e)).wait_recv()
 
     def state_copy():
         return remote(passed, came, ssend.at[0], srecv.at[0], (z + 1, e))
@@ -591,10 +591,10 @@
         return carry
 
     def exchange(n):
-        return remote(acc.at[n, theirs], swap.at[n], xsend.at[n], xrecv.at[n], partner)
+        return remote(acc.at[n, theirs], swap.at[n], xsend.at[0], xrecv.at[n], partner)
 
     def bring_home(n):
-        return remote(acc.at[n, mine], ret.at[n - 2], bsend.at[n], brecv.at[n], peer(n // 2, half))
+        return remote(acc.at[n, mine], ret.at[n - 2], bsend.at[0], brecv.at[0], peer(n // 2, half))
 
     def finish(n):
         exchange(n).wait_recv()
@@ -726,19 +726,19 @@
             own_in(n).start()
 
     def exchange2(k):
-        return remote(acc2.at[k, :, theirs], swap2.at[k], x2send.at[k], x2recv.at[k], partner)
+        return remote(acc2.at[k, :, theirs], swap2.at[k], x2send.at[0], x2recv.at[k], partner)
 
     def bring_home2(k, c):
         return remote(
             acc2.at[k, pl.ds(2 * c, 2), mine],
             ret2.at[k, c - 1],
-            b2send.at[k, c],
-            b2recv.at[k, c],
+            b2send.at[0],
+            b2recv.at[k],
             peer(c, half),
         )
 
     def edge_copy(k):
-        return remote(edge.at[k], edge.at[k], rsend.at[k], rrecv.at[k], (outer, e))
+        return remote(edge.at[k], edge.at[k], rsend.at[0], rrecv.at[0], (outer, e))
 
     def helper_dot(k):
         for i in range(GROUPS):
@@ -760,8 +760,9 @@
             bring_home2(k, c).start()
 
     def helper_edge(k):
-        for c in range(1, CHUNKS - 1):
-            bring_home2(k, c).wait_recv()
+        remote(
+            ret2.at[k], ret2.at[k], b2send.at[0], b2recv.at[k], peer(1, half)
+        ).wait_recv()
         for h in range(2):
             total = share[h, :, 0:1] * acc2[k, h, mine]
             for c in range(1, CHUNKS - 1):
@@ -852,18 +853,21 @@
 
     lax.fori_loop(0, GROUPS + 7, finish_step, 0)
 
+    returned = remote(ret, ret, bsend.at[0], brecv.at[0], peer(1, half))
+    returned.wait_recv()
     for h in range(2):
         total = share[h, :, 0:1] * acc[h, mine]
         for c in range(1, CHUNKS):
             n = 2 * c + h
-            bring_home(n).wait_recv()
             total += share[n, :, 0:1] * ret[n - 2]
         swap[h] = total
 
+    edges = remote(edge, edge, rsend.at[0], rrecv.at[0], (near, e))
+
     @pl.when(end)
     def _():
+        edges.wait_recv()
         for k in range(GROUPS):
-            edge_copy(k).wait_recv()
             span = pl.ds(k * wide, wide)
             for h in range(2):
                 line = pl.ds(h * sub, sub)
@@ -879,32 +883,27 @@
     def _():
         state_copy().wait_send()
 
-    for copy in (*to_partner, *to_x, *to_y, *pass_x, *pass_y, *across.values()):
-        copy.wait_send()
-    for n in range(UNITS):
-        own_in(n).wait_send()
-        exchange(n).wait_send()
-        if n > 1:
-            bring_home(n).wait_send()
+    def sent(ref, ssem, device):
+        remote(ref, ref, ssem.at[0], hrecv.at[0, 0], device).wait_send()
+
+    sent(tok.at[pl.ds(0, UNITS - 1)], tsend, partner)
+    sent(hid.at[z], own_in_send, (inner, e))
+    sent(swap, xsend, partner)
+    returned.wait_send()
 
     @pl.when(inside)
     def _():
-        for n in range(UNITS):
-            own_out(n).wait_send()
-            fwd_in(n).wait_send()
-            fwd_out(n).wait_send()
-        for k in range(GROUPS):
-            exchange2(k).wait_send()
-            edge_copy(k).wait_send()
-            for c in range(1, CHUNKS - 1):
-                bring_home2(k, c).wait_send()
-        for n in range(HELPED, UNITS):
-            fwd_end(n).wait_send()
+        sent(hid.at[z], own_out_send, (outer, e))
+        sent(hid.at[near], fwd_in_send, (inner, e))
+        sent(hid.at[far], fwd_out_send, (outer, e))
+        sent(hid.at[opposite, pl.ds(HELPED, UNITS - HELPED)], fwd_end_send, (outer, e))
+        sent(swap2, x2send, partner)
+        sent(ret2, b2send, partner)
+        edges.wait_send()
 
     @pl.when(end)
     def _():
-        for k in range(GROUPS):
-            lend(k).wait_send()
+        sent(far_w, wsend, (inner, e))
 
     mix_copy.wait()
     out_copy.wait()
@@ -976,26 +975,26 @@
             pltpu.VMEM((state_count, lanes), F32),
             dma((9,)),
             dma((8,)),
+            dma((1,)),
             dma((16,)),
-            dma((16,)),
+            dma((1,)),
+            dma((1,)),
+            dma((1,)),
+            dma((1,)),
+            dma((1,)),
+            dma((3, UNITS)),
+            dma((1,)),
+            dma((GROUPS,)),
+            dma((1,)),
+            dma((1,)),
+            dma((1,)),
             dma((UNITS,)),
-            dma((UNITS,)),
-            dma((UNITS,)),
-            dma((UNITS,)),
-            dma((2,)),
-            dma((3, UNITS)),
+            dma((1,)),
+            dma((1,)),
+            dma((1,)),
             dma((GROUPS,)),
+            dma((1,)),
             dma((GROUPS,)),
-            dma((GROUPS,)),
-            dma((GROUPS,)),
-            dma((UNITS,)),
-            dma((UNITS,)),
-            dma((UNITS,)),
-            dma((UNITS,)),
-            dma((GROUPS,)),
-            dma((GROUPS,)),
-            dma((GROUPS, CHUNKS)),
-            dma((GROUPS, CHUNKS)),
             dma((1,)),
             dma((1,)),
         ],

time: 110 us -> 108 us (0.982)
    pallas_call x1, Pallas kernels: 107 us -> 106 us  [fused(): pl.pallas_call(fused_kernel, out_shape=(jax.ShapeDtypeStruct(seq_inputs.s...]
where the time goes in v4:
time: 108 us
  Pallas kernels  108 us (100%)
    pallas_call x1, Pallas kernels, fused(): pl.pallas_call(fused_kernel, out_shape=(jax.ShapeDtypeStruct(seq_inputs.s...  106 us

profile of v4, /device:TPU:0, one launch (start us, length us, event | category | flops | bytes accessed | tf_op | source)
XLA Modules:
  0.0 108.2 jit_solution(13543422643670865890)
XLA Ops:
  0.6 105.8 %shard_map.131 = (bf16[512,256]{1,0:T(8,128)(2,1)}, bf16[128,1024]{1,0:T(8,128)(2,1)}) custom-call(bf16[128,4096]{1,0:T(8,128)(2,1)} %tok_hbm.1, s32[2,128]{1,0:T(2,128)} %bitcast.8, f32[2,128]{1,0:T(2,128)} %bitcast.9, bf16[512,256]{1,0:T(8,128)(2,1)} %seq_hbm.1, f32[4,512]{1,0:T(4,128)} %step_hbm.1, bf16[16,512]{1,0:T(8,128)(2,1)} %write_hbm.1, ...), custom_call_target="tpu_custom_call" | custom-call | tf_op jit(solution)/shard_map/pallas_call | solution.py:936
  106.4 1.8 %shard_map.132 = (bf16[512,256]{1,0:T(8,128)(2,1)}, bf16[128,1024]{1,0:T(8,128)(2,1)}) custom-call(bf16[512,256]{1,0:T(8,128)(2,1)} %get-tuple-element.4.refs_0_, bf16[128,1024]{1,0:T(8,128)(2,1)} %get-tuple-element.5.refs_1_), custom_call_target="tpu_custom_call" | custom-call | tf_op jit(solution)/shard_map/pallas_call | solution.py:1050

commit v5 on v4

--- a/solution.py
+++ b/solution.py
@@ -281,19 +281,22 @@
             ]
         )
     ]
+    barrier = pltpu.get_barrier_semaphore()
+    for device in (partner, peer(1, half), peer(2, half), peer(3, half)):
+        pl.semaphore_signal(barrier, inc=1, device_id=device, device_id_type=MESH)
+    pl.semaphore_signal(barrier, inc=1, device_id=(inner, e), device_id_type=MESH)
+
+    @pl.when(inside)
+    def _():
+        pl.semaphore_signal(barrier, inc=1, device_id=(outer, e), device_id_type=MESH)
+
     for load in loads[:6]:
         load.start()
     for load in small:
         load.start()
 
-    barrier = pltpu.get_barrier_semaphore()
-    for device in (partner, peer(1, half), peer(2, half), peer(3, half)):
-        pl.semaphore_signal(barrier, inc=1, device_id=device, device_id_type=MESH)
-    pl.semaphore_signal(barrier, inc=1, device_id=(inner, e), device_id_type=MESH)
-
     @pl.when(inside)
     def _():
-        pl.semaphore_signal(barrier, inc=1, device_id=(outer, e), device_id_type=MESH)
         pl.semaphore_wait(barrier, 6)
 
     @pl.when(end)
@@ -640,7 +643,8 @@
 
                         @pl.when(inside)
                         def _():
-                            take_near(1)
+                            arrived(0, near, 1)
+                            fwd_in(1).start()
 
             @pl.when(t == 0)
             def _():
@@ -711,6 +715,10 @@
         @pl.when(inside & (t > 3))
         def _():
             take_near(unit_of(t - 2))
+
+        @pl.when(inside & (t == 2))
+        def _():
+            add_down(near, 1)
 
         @pl.when(inside & ((t == 4) | (t == 6)))
         def _():

time: 108 us -> 108 us (level)
  no operation moved by 1% of the time
where the time goes in v5:
time: 108 us
  Pallas kernels  108 us (100%)
    pallas_call x1, Pallas kernels, fused(): pl.pallas_call(fused_kernel, out_shape=(jax.ShapeDtypeStruct(seq_inputs.s...  106 us

profile of v5, /device:TPU:0, one launch (start us, length us, event | category | flops | bytes accessed | tf_op | source)
XLA Modules:
  0.0 108.2 jit_solution(9868821948170704227)
XLA Ops:
  0.6 105.7 %shard_map.131 = (bf16[512,256]{1,0:T(8,128)(2,1)}, bf16[128,1024]{1,0:T(8,128)(2,1)}) custom-call(bf16[128,4096]{1,0:T(8,128)(2,1)} %tok_hbm.1, s32[2,128]{1,0:T(2,128)} %bitcast.8, f32[2,128]{1,0:T(2,128)} %bitcast.9, bf16[512,256]{1,0:T(8,128)(2,1)} %seq_hbm.1, f32[4,512]{1,0:T(4,128)} %step_hbm.1, bf16[16,512]{1,0:T(8,128)(2,1)} %write_hbm.1, ...), custom_call_target="tpu_custom_call" | custom-call | tf_op jit(solution)/shard_map/pallas_call | solution.py:944
  106.4 1.8 %shard_map.132 = (bf16[512,256]{1,0:T(8,128)(2,1)}, bf16[128,1024]{1,0:T(8,128)(2,1)}) custom-call(bf16[512,256]{1,0:T(8,128)(2,1)} %get-tuple-element.4.refs_0_, bf16[128,1024]{1,0:T(8,128)(2,1)} %get-tuple-element.5.refs_1_), custom_call_target="tpu_custom_call" | custom-call | tf_op jit(solution)/shard_map/pallas_call | solution.py:1058
